TPU v7x, 128 devices: a whole 4x4x4 slice. The times are simulated.
128 devices in a mesh: dp: 8 (over y, x_hi), mp: 16 (over z, x_lo, core).
Axes of the slice: x: 4 (x_hi: 2, x_lo: 2; x = x_hi * 2 + x_lo), y: 4, z: 4, core: 2. Of those that a mesh axis runs over, the one named last changes fastest.
Arguments:
- emb_grad: bfloat16 [76032, 3584], P('mp', 'dp'), may hold values from -70 to 70
- emb_mom: bfloat16 [16, 8, 8, 594, 448], P('mp', None, 'dp'), may hold values from -0.29882812 to 0.29882812
- blk_grad: bfloat16 [2, 3584, 18944], P(None, 'dp', 'mp'), may hold values from -70 to 70
- blk_mom: bfloat16 [2, 16, 3584, 1184], P(None, None, ('dp', 'mp')), may hold values from -0.29882812 to 0.29882812
- tile_group: int32 [2, 16, 16], replicated, may hold values from 1 to 3
- clip_rms: float32 [4], replicated, may hold values from 0.05 to 80
Outputs:
- emb_update: bfloat16 [16, 8, 8, 594, 448], P('mp', None, 'dp')
- emb_moment: bfloat16 [16, 8, 8, 594, 448], P('mp', None, 'dp')
- blk_update: bfloat16 [2, 16, 3584, 1184], P(None, None, ('dp', 'mp'))
- blk_moment: bfloat16 [2, 16, 3584, 1184], P(None, None, ('dp', 'mp'))
All inputs are finite; a program needn't handle non-finite values.
Results may differ from a plain program's by a relative error of at most 0.001.
Values may be sent and summed in bfloat16 or wider, within the bound.
No kernel may reach another device: no remote copies, remote signals or barrier semaphores. Data moves between devices by JAX's collectives and lax.ppermute only.
A program may use at most 128 MiB of HBM per device.

v0:
```python
import functools

import jax
import jax.numpy as jnp
from jax import lax
from jax.sharding import Mesh
from jax.sharding import PartitionSpec as P

DP = ("dp_0", "dp_1")
MP = ("mp_0", "mp_1", "mp_2")
DP_MP = ("dp_0", "dp_1", "mp_0", "mp_1", "mp_2")


beta_first = 0.9
beta_second = 0.99
temper = 0.05
epsilon = 1e-06


def one_axis_at_a_time(shard, axes):
    return functools.reduce(lax.psum, axes, shard)


def lion_step(clipped, moment):
    moment = moment.astype(jnp.float32)
    update = jnp.tanh((beta_first * moment + (1.0 - beta_first) * clipped) / temper).astype(
        jnp.bfloat16
    )
    new_moment = (beta_second * moment + (1.0 - beta_second) * clipped).astype(jnp.bfloat16)
    return (update, new_moment)


def on_device(emb_grad, emb_mom, blk_grad, blk_mom, tile_group, clip_rms):
    dp_count = lax.axis_size(DP)
    mp_count = lax.axis_size(MP)
    dp_index = lax.axis_index(DP)
    mp_index = lax.axis_index(MP)
    groups = clip_rms.shape[0]
    tile_rows, tile_cols = emb_grad.shape
    own_rows = emb_mom.shape[3]
    feature_block = emb_mom.shape[4]
    matrices, block_rows, block_cols = blk_grad.shape
    owner_rows = blk_mom.shape[2]
    row_blocks = tile_group.shape[1] // dp_count
    block_height = block_rows // row_blocks
    labels = jnp.arange(groups, dtype=jnp.int32)
    first = (labels == 0).astype(jnp.float32)
    onehot = (tile_group[..., None] == labels).astype(jnp.float32)
    counts = jnp.sum(onehot, axis=(0, 1, 2)) * float(block_height * block_cols) + first * float(
        tile_rows * mp_count * tile_cols * dp_count
    )
    owner_block = dp_index * row_blocks + mp_index * owner_rows // block_height
    owner_ids = lax.dynamic_index_in_dim(onehot, owner_block, axis=1, keepdims=False)
    grad_pieces = blk_grad.reshape(matrices, mp_count, owner_rows, block_cols)
    blk_owner = lax.all_to_all(grad_pieces, MP, split_axis=1, concat_axis=1, tiled=True)
    emb_pieces = emb_grad.reshape(dp_count, own_rows, feature_block)
    mom_local = emb_mom.reshape(dp_count, own_rows, feature_block)
    emb_owner = lax.all_to_all(emb_pieces, DP, split_axis=0, concat_axis=0, tiled=True)
    emb_squares = jnp.sum(jnp.square(emb_grad.astype(jnp.float32)))
    block_squares = jnp.sum(
        jnp.square(blk_grad.astype(jnp.float32)).reshape(
            matrices, row_blocks, block_height, block_cols
        ),
        axis=(2, 3),
    )
    tile_rows_ids = lax.dynamic_slice_in_dim(onehot, dp_index * row_blocks, row_blocks, axis=1)
    tile_ids = lax.dynamic_index_in_dim(tile_rows_ids, mp_index, axis=2, keepdims=False)
    block_terms = jnp.sum(block_squares[..., None] * tile_ids, axis=(0, 1))
    partial_value = block_terms + emb_squares * first
    totals = one_axis_at_a_time(partial_value, DP_MP)
    root_mean = jnp.sqrt(totals / jnp.maximum(counts, 1.0))
    factor = jnp.minimum(1.0, clip_rms / (root_mean + epsilon))
    owner_factor = jnp.sum(owner_ids * factor, axis=-1)
    clipped = blk_owner.astype(jnp.float32) * owner_factor[:, :, None, None]
    blk_update, blk_moment = lion_step(clipped, blk_mom)
    emb_update, emb_moment = lion_step(emb_owner.astype(jnp.float32) * factor[0], mom_local)
    return (
        emb_update.reshape(emb_mom.shape),
        emb_moment.reshape(emb_mom.shape),
        blk_update,
        blk_moment,
    )


def solution(mesh):
    torus = Mesh(mesh.devices.reshape(4, 2, 4, 2, 2), ("dp_0", "dp_1", "mp_0", "mp_1", "mp_2"))
    return jax.shard_map(
        on_device,
        mesh=torus,
        in_specs=(
            P(MP, DP),
            P(MP, None, DP, None, None),
            P(None, DP, MP),
            P(None, None, DP_MP, None),
            P(),
            P(),
        ),
        out_specs=(
            P(MP, None, DP, None, None),
            P(MP, None, DP, None, None),
            P(None, None, DP_MP, None),
            P(None, None, DP_MP, None),
        ),
        check_vma=False,
    )
```

profile of v0, /device:TPU:1, one launch (start us, length us, event | category | flops | bytes accessed | tf_op | source)
XLA Modules:
  0.0 140.6 jit_solution(2279655981874560583)
XLA Ops:
  0.6 5.4 %copy.51 = bf16[2,448,1184]{2,0,1:T(2,128)(2,1)} copy(bf16[2,448,1184]{2,1,0:T(8,128)(2,1)} %param.8) | data formatting | bytes 4243456 | tf_op args[2]
  6.0 7.7 %all-to-all-start.1 = ((bf16[2,16,28,1184]{3,0,2,1:T(2,128)(2,1)}), bf16[2,16,28,1184]{3,0,2,1:T(2,128)(2,1)S(1)}, u32[]{:S(2)}, u32[]{:S(2)}) async-start(bf16[2,16,28,1184]{3,0,2,1:T(2,128)(2,1)} %bitcast.40), calls=%async_computation.1 | async-start | bytes 4587520 | tf_op jit(solution)/shard_map/all_to_all | solution.py:55
  13.8 9.5 %reshape.32 = bf16[8,594,448]{1,0,2:T(8,128)(2,1)} reshape(bf16[4752,448]{0,1:T(8,128)(2,1)} %param.6) | data formatting | bytes 8515584 | tf_op jit(solution)/shard_map/reshape | solution.py:56
  23.2 5.0 %copy.50 = bf16[8,594,448]{1,2,0:T(8,128)(2,1)} copy(bf16[8,594,448]{1,0,2:T(8,128)(2,1)} %reshape.32) | data formatting | bytes 8515584 | tf_op jit(solution)/shard_map/reshape | solution.py:56
  28.3 0.0 copy-start
  28.3 14.5 %all-to-all-done.1 = bf16[2,16,28,1184]{3,0,2,1:T(2,128)(2,1)S(1)} async-done(((bf16[2,16,28,1184]{3,0,2,1:T(2,128)(2,1)}), bf16[2,16,28,1184]{3,0,2,1:T(2,128)(2,1)S(1)}, u32[]{:S(2)}, u32[]{:S(2)}) %all-to-all-start.1) | async-done | bytes 2121760 | tf_op jit(solution)/shard_map/all_to_all | solution.py:55
  42.8 6.4 %all-to-all-start = ((bf16[8,594,448]{1,2,0:T(8,128)(2,1)}), bf16[8,594,448]{1,2,0:T(8,128)(2,1)}, u32[]{:S(2)}, u32[]{:S(2)}) async-start(bf16[8,594,448]{1,2,0:T(8,128)(2,1)} %copy.50), calls=%async_computation | async-start | bytes 9175040 | tf_op jit(solution)/shard_map/all_to_all | solution.py:58
  49.2 0.0 copy-start.1
  49.2 2.2 %multiply_reduce_fusion.1 = f32[2,448]{1,0:T(2,128)S(1)} fusion(bf16[2,448,1184]{2,1,0:T(8,128)(2,1)} %param.8), kind=kLoop, calls=%fused_computation.23 | loop fusion | flops 3181696 | bytes 2125312 | tf_op jit(solution)/shard_map/reduce_sum | solution.py:60
  51.4 0.1 reduce_sum.53
  51.5 0.1 reduce_sum.54
  51.6 0.0 copy-done
  51.6 0.2 dynamic-slice_reduce_fusion
  51.7 0.1 multiply_reduce_fusion.2
  51.8 5.1 %multiply_reduce_fusion = f32[]{:T(128)} fusion(bf16[4752,448]{0,1:T(8,128)(2,1)} %param.6), kind=kLoop, calls=%fused_computation.11 | loop fusion | flops 6386687 | bytes 4257796 | tf_op jit(solution)/shard_map/reduce_sum | solution.py:59
  56.9 0.6 fusion.19
  57.6 42.9 %psum.35 = f32[4]{0:T(128)S(1)} all-reduce(f32[4]{0:T(128)S(1)} %fusion.19), channel_id=1, replica_groups=mesh['dp_0'=4,'dp_1'=2,'mp_0'=4,'mp_1'=2,'mp_2'=2] {'dp_0'}, use_global_device_ids=true, to_apply=%region_4.5 | all-reduce | flops 4 | bytes 32 | tf_op jit(solution)/shard_map/psum | solution.py:21
  100.5 7.4 %psum.36 = f32[4]{0:T(128)S(1)} all-reduce(f32[4]{0:T(128)S(1)} %psum.35), channel_id=1, replica_groups=mesh['dp_0'=4,'dp_1'=2,'mp_0'=4,'mp_1'=2,'mp_2'=2] {'dp_1'}, use_global_device_ids=true, to_apply=%region_5.6 | all-reduce | flops 4 | bytes 32 | tf_op jit(solution)/shard_map/psum | solution.py:21
  107.9 7.2 %psum.37 = f32[4]{0:T(128)S(1)} all-reduce(f32[4]{0:T(128)S(1)} %psum.36), channel_id=1, replica_groups=mesh['dp_0'=4,'dp_1'=2,'mp_0'=4,'mp_1'=2,'mp_2'=2] {'mp_0'}, use_global_device_ids=true, to_apply=%region_6.7 | all-reduce | flops 4 | bytes 32 | tf_op jit(solution)/shard_map/psum | solution.py:21
  115.1 3.8 %psum.38 = f32[4]{0:T(128)S(1)} all-reduce(f32[4]{0:T(128)S(1)} %psum.37), channel_id=1, replica_groups=mesh['dp_0'=4,'dp_1'=2,'mp_0'=4,'mp_1'=2,'mp_2'=2] {'mp_1'}, use_global_device_ids=true, to_apply=%region_7.8 | all-reduce | flops 4 | bytes 32 | tf_op jit(solution)/shard_map/psum | solution.py:21
  118.9 8.6 %psum.39 = f32[4]{0:T(128)S(1)} all-reduce(f32[4]{0:T(128)S(1)} %psum.38), channel_id=1, replica_groups=mesh['dp_0'=4,'dp_1'=2,'mp_0'=4,'mp_1'=2,'mp_2'=2] {'mp_2'}, use_global_device_ids=true, to_apply=%region_8.9 | all-reduce | flops 4 | bytes 32 | tf_op jit(solution)/shard_map/psum | solution.py:21
  127.5 0.1 fusion.17
  127.6 0.0 copy-done.1
  127.7 0.1 fusion.18
  127.7 4.7 %fusion.13 = (bf16[2,16,28,1184]{3,1,2,0:T(8,128)(2,1)}, bf16[2,16,28,1184]{3,1,2,0:T(8,128)(2,1)}) fusion(bf16[2,16,28,1184]{3,1,2,0:T(8,128)(2,1)} %param.9, f32[2,16]{1,0:T(2,128)S(1)} %fusion.18, bf16[2,16,28,1184]{3,0,2,1:T(2,128)(2,1)S(1)} %all-to-all-done.1), kind=kLoop, calls=%fused_computation.19 | loop fusion | flops 12730368 | bytes 8487040 | tf_op jit(solution)/shard_map/convert_element_type | solution.py:29
  132.5 0.0 all-to-all-done
  132.5 8.2 %fusion.14 = (bf16[1,8,1,594,448]{3,4,2,1,0:T(8,128)(2,1)}, bf16[1,8,1,594,448]{3,4,2,1,0:T(8,128)(2,1)}) fusion(bf16[8,594,448]{1,2,0:T(8,128)(2,1)} %all-to-all-done, bf16[1,8,1,594,448]{3,4,2,1,0:T(8,128)(2,1)} %param.7, f32[]{:T(128)S(1)} %bitcast.41), kind=kLoop, calls=%fused_computation.20 | loop fusion | flops 25546752 | bytes 17031172
  (2 shorter events, 0.0 us)
Async XLA Ops:
  6.0 36.8 %all-to-all-start.1 = ((bf16[2,16,28,1184]{3,0,2,1:T(2,128)(2,1)}), bf16[2,16,28,1184]{3,0,2,1:T(2,128)(2,1)S(1)}, u32[]{:S(2)}, u32[]{:S(2)}) async-start(bf16[2,16,28,1184]{3,0,2,1:T(2,128)(2,1)} %bitcast.40), calls=%async_computation.1 | async-start | bytes 4587520 | tf_op jit(solution)/shard_map/all_to_all | solution.py:55
  28.3 23.3 %copy-start = (s32[2,16,16]{2,1,0:T(8,128)S(1)}, s32[2,16,16]{2,1,0:T(8,128)}, u32[]{:S(2)}) copy-start(s32[2,16,16]{2,1,0:T(8,128)} %param.10) | copy-start | bytes 6148
  42.8 89.6 %all-to-all-start = ((bf16[8,594,448]{1,2,0:T(8,128)(2,1)}), bf16[8,594,448]{1,2,0:T(8,128)(2,1)}, u32[]{:S(2)}, u32[]{:S(2)}) async-start(bf16[8,594,448]{1,2,0:T(8,128)(2,1)} %copy.50), calls=%async_computation | async-start | bytes 9175040 | tf_op jit(solution)/shard_map/all_to_all | solution.py:58
  49.2 78.5 %copy-start.1 = (f32[4]{0:T(128)S(1)}, f32[4]{0:T(128)}, u32[]{:S(2)}) copy-start(f32[4]{0:T(128)} %param.11) | copy-start | bytes 52
where the time goes:
time: 141 us
  blocking collectives  69.9 us (50%)
  other arithmetic  21.2 us (15%)
  local copies, waits for them, and re-layouts  20.1 us (14%)
  waiting for transfers between devices  14.5 us (10%)
  starting transfers between devices  14.1 us (10%)
    psum x5, blocking collectives, one_axis_at_a_time(): return functools.reduce(lax.psum, axes, shard)  69.9 us
    all_to_all x1, waiting for transfers between devices, on_device(): lax.all_to_all(grad_pieces, MP, split_axis=1, concat_axis=1, tiled=True)  14.5 us
    reshape x2, local copies, waits for them, and re-layouts, on_device(): emb_pieces = emb_grad.reshape(dp_count, own_rows, feature_block)  14.5 us
    unnamed x1, other arithmetic  8.16 us
    all_to_all x1, starting transfers between devices, on_device(): lax.all_to_all(grad_pieces, MP, split_axis=1, concat_axis=1, tiled=True)  7.75 us
    all_to_all x1, starting transfers between devices, on_device(): lax.all_to_all(emb_pieces, DP, split_axis=0, concat_axis=0, tiled=True)  6.36 us
    unnamed x5, local copies, waits for them, and re-layouts  5.4 us
    reduce_sum x1, other arithmetic, on_device(): emb_squares = jnp.sum(jnp.square(emb_grad.astype(jnp.float32)))  5.08 us
  transfers between devices with their start and end apart: 2, of which 1 were waited for; matrix products, arithmetic and copies ran while one was open for 20% of the time, Pallas kernels for 0%

commit v1 on v0

v1 whole, which is shorter than its diff:
```python
import functools

import jax
import jax.numpy as jnp
from jax import lax
from jax.experimental import pallas as pl
from jax.experimental.pallas import tpu as pltpu
from jax.sharding import Mesh
from jax.sharding import PartitionSpec as P


DP = ("dp_0", "dp_1")
MP = ("mp_0", "mp_1", "mp_2")
DP_MP = DP + MP


beta_first = 0.9
beta_second = 0.99
temper = 0.05
epsilon = 1e-06

VMEM_BYTES = 67_043_328
LION_BYTES = 24 * 1024 * 1024
F32 = jnp.float32
BF16 = jnp.bfloat16
ANY = pl.BlockSpec(memory_space=pltpu.HBM)
VMEM = pl.BlockSpec(memory_space=pltpu.VMEM)
SMEM = pl.BlockSpec(memory_space=pltpu.SMEM)

EMB_ROWS = 2080
BLK_ROWS = 520
SUM_ROW = 512
SUM_LANE = 96


EMB_STEPS = [(0, 1), (1, 0), (1, 1), (2, 0), (2, 1), (3, 0), (3, 1), (0, 0)]


def emb_peer(a, b, step, sign):
    return ((a + sign * step[0] + 4) % 4) * 2 + (b ^ step[1])


def lanes(shape):
    return lax.broadcasted_iota(jnp.int32, shape, len(shape) - 1)


def split_three(value):
    high = value.astype(BF16).astype(F32)
    middle = (value - high).astype(BF16).astype(F32)
    low = (value - high - middle).astype(BF16).astype(F32)
    return high, middle, low


def fold8(x):
    return jnp.sum(x.reshape(x.shape[0] // 8, 8, x.shape[1]), axis=0)


def emb_peers(sign):
    a, b = (lax.axis_index(name) for name in DP)
    return [emb_peer(a, b, step, sign) for step in EMB_STEPS]


def blk_pack_kernel(groups, label_ref, grad, emb, *rest):
    dp_index = lax.axis_index("dp_0") * 2 + lax.axis_index("dp_1")
    mp_index = lax.axis_index("mp_0") * 4 + lax.axis_index("mp_1") * 2 + lax.axis_index("mp_2")
    out, stage, xb, xe, bsem, esem, osem = rest
    matrices, block_rows, block_cols = xb.shape
    count = stage.shape[0]
    owner_rows = block_rows // count
    half = block_rows // 2
    step = 64
    steps = xe.shape[0] // step
    for m in range(matrices):
        pltpu.make_async_copy(grad.at[m], xb.at[m], bsem.at[m]).start()
    for g in range(steps):
        pltpu.make_async_copy(
            emb.at[pl.ds(g * step, step)], xe.at[pl.ds(g * step, step)], esem.at[g]
        ).start()
    full = block_cols // 128
    for m in range(matrices):
        pltpu.make_async_copy(grad.at[m], xb.at[m], bsem.at[m]).wait()
    block_sums = []
    for m in range(matrices):
        for h in range(2):
            x = xb[m, h * half : (h + 1) * half, :].astype(F32)
            block_sums.append(jnp.sum(fold8(x * x)))
    for j in range(count):
        x = jnp.concatenate(
            [xb[m, j * owner_rows : (j + 1) * owner_rows, :].astype(F32) for m in range(matrices)],
            axis=0,
        )
        rows = x.shape[0]
        for t in range(full):
            stage[j, t * rows : (t + 1) * rows, :] = x[:, t * 128 : (t + 1) * 128].astype(BF16)
        tail = x[:, full * 128 :]
        for q in range(4):
            part = tail[q * 16 : min(q * 16 + 16, rows), :].astype(BF16)
            base = rows * full
            stage[j, base : base + part.shape[0], q * 32 : (q + 1) * 32] = part
    acc = jnp.zeros((8, 512), F32)
    tail_acc = jnp.zeros((8, xe.shape[1] % 512), F32)
    for g in range(steps):
        pltpu.make_async_copy(
            emb.at[pl.ds(g * step, step)], xe.at[pl.ds(g * step, step)], esem.at[g]
        ).wait()
        for c in range(xe.shape[1] // 512):
            x = xe[g * step : (g + 1) * step, c * 512 : (c + 1) * 512].astype(F32)
            acc = acc + fold8(x * x)
        x = xe[g * step : (g + 1) * step, xe.shape[1] // 512 * 512 :].astype(F32)
        tail_acc = tail_acc + fold8(x * x)
    emb_sum = jnp.sum(acc) + jnp.sum(tail_acc)
    lane = lanes((8, 128))
    sums = jnp.zeros((8, 128), F32)
    for g in range(groups):
        total = emb_sum if g == 0 else jnp.float32(0)
        for i, s in enumerate(block_sums):
            label = label_ref[i // 2, dp_index * 2 + i % 2, mp_index]
            total = total + jnp.where(label == g, s, jnp.float32(0))
        for p, piece in enumerate(split_three(jnp.full((8, 128), total, F32))):
            sums = jnp.where(lane == SUM_LANE + 3 * g + p, piece, sums)
    for j in range(count):
        old = stage[j, SUM_ROW:, :].astype(F32)
        stage[j, SUM_ROW:, :] = jnp.where(lane < SUM_LANE, old, sums).astype(BF16)
    copy = pltpu.make_async_copy(stage, out, osem.at[0])
    copy.start()
    copy.wait()


def emb_pack_kernel(emb, *rest):
    dest = emb_peers(1)
    outs, (stage, xe, esem, osem) = rest[:8], rest[8:]
    features, tile_rows = xe.shape
    count = stage.shape[0]
    own_rows = tile_rows // count
    step = 64
    steps = features // step
    full = own_rows // 128
    rest_lanes = own_rows - full * 128 - 64
    for g in range(steps):
        pltpu.make_async_copy(
            emb.at[pl.ds(g * step, step)], xe.at[pl.ds(g * step, step)], esem.at[g]
        ).start()
    lane = lanes((step, 128))
    low = lanes((step // 2, 128)) < 64
    for g in range(steps):
        pltpu.make_async_copy(
            emb.at[pl.ds(g * step, step)], xe.at[pl.ds(g * step, step)], esem.at[g]
        ).wait()

        def tile(i):
            x = xe[g * step : (g + 1) * step, i * 128 : min(i * 128 + 128, tile_rows)].astype(F32)
            if x.shape[1] < 128:
                x = jnp.concatenate([x, jnp.zeros((step, 128 - x.shape[1]), F32)], axis=1)
            return x

        for d in range(count):
            q, r = divmod(d * own_rows, 128)
            need = -(-(r + own_rows) // 128)
            turned = [pltpu.roll(tile(q + i), (128 - r) % 128, 1) if r else tile(q + i) for i in range(need)]
            for t in range(full + 1):
                x = turned[t]
                if r and t + 1 < need:
                    x = jnp.where(lane < 128 - r, x, turned[t + 1])
                if t < full:
                    stage[d, t * features + g * step : t * features + (g + 1) * step, :] = x.astype(BF16)
            half = step // 2
            both = jnp.where(low, x[:half], pltpu.roll(x[half:], 64, 1))
            base = full * features
            stage[d, base + g * half : base + (g + 1) * half, :] = both.astype(BF16)
            base = base + features // 2
            moved = pltpu.roll(x, (rest_lanes * g + 64) % 128, 1)
            if g:
                old = stage[d, base:, :].astype(F32)
                moved = jnp.where(lane < rest_lanes * g, old, moved)
            stage[d, base:, :] = moved.astype(BF16)
    copies = [
        pltpu.make_async_copy(stage.at[dest[k]], out, osem.at[k]) for k, out in enumerate(outs)
    ]
    for c in copies:
        c.start()
    for c in copies:
        c.wait()


def step_of(grad, factor, moment):
    clipped = grad * factor
    update = jnp.tanh((beta_first * moment + (1.0 - beta_first) * clipped) / temper)
    return update.astype(BF16), (beta_second * moment + (1.0 - beta_second) * clipped).astype(BF16)


def blk_lion_kernel(factor_ref, *rest):
    stage, mv, update, moment, wide, uv, nv, osem = rest
    count, mom = stage.shape[0], mv
    matrices, owner_rows, _, block_cols = mom.shape
    rows = matrices * owner_rows
    full = block_cols // 128
    for s in range(count):
        for m in range(matrices):
            f = factor_ref[m, s]
            for t in range(full):
                x = stage[s, t * rows + m * owner_rows : t * rows + (m + 1) * owner_rows, :].astype(F32)
                wide[t, pl.ds(m * owner_rows * count + s, owner_rows, stride=count), :] = x * f
        tail = []
        for q in range(4):
            n = min(16, rows - q * 16)
            x = stage[s, rows * full : rows * full + 16, :].astype(F32)
            tail.append((pltpu.roll(x, 128 - 32 * q, 1) if q else x)[:n])
        tail = jnp.concatenate(tail, axis=0)
        for m in range(matrices):
            f = factor_ref[m, s]
            wide[full, pl.ds(m * owner_rows * count + s, owner_rows, stride=count), :] = (
                tail[m * owner_rows : (m + 1) * owner_rows] * f
            )
    for m in range(matrices):
        for r in range(owner_rows):
            base = (m * owner_rows + r) * count
            for t in range(full + 1):
                cols = slice(t * 128, min(t * 128 + 128, block_cols))
                grad = wide[t, base : base + count, : cols.stop - cols.start]
                up, new = step_of(grad, 1.0, mv[m, r, :, cols].astype(F32))
                uv[m, r, :, cols] = up
                nv[m, r, :, cols] = new
        pltpu.make_async_copy(uv.at[m], update.at[m], osem.at[m]).start()
        pltpu.make_async_copy(nv.at[m], moment.at[m], osem.at[2 + m]).start()
    for m in range(matrices):
        pltpu.make_async_copy(uv.at[m], update.at[m], osem.at[m]).wait()
        pltpu.make_async_copy(nv.at[m], moment.at[m], osem.at[2 + m]).wait()


def emb_lion_kernel(which, chained, factor_ref, *rest):
    n = len(which)
    source = [emb_peers(-1)[i] for i in which]
    parts, rest = rest[:n], rest[n:]
    mom, rest = rest[0], rest[1:]
    if chained:
        rest = rest[2:]
    update, moment, uv, nv, usem, nsem = rest
    _, features, own_rows = mom.shape
    step = 64
    full = own_rows // 128
    rest_lanes = own_rows - full * 128 - 64
    f = factor_ref[0]
    low = lanes((step, 128)) < 64
    for k in range(n):
        for g in range(features // step):
            rows = slice(g * step, (g + 1) * step)
            for t in range(full + 1):
                cols = slice(t * 128, min(t * 128 + 128, own_rows))
                if t < full:
                    x = parts[k][t * features + g * step : t * features + (g + 1) * step, :].astype(F32)
                else:
                    half = step // 2
                    base = full * features
                    both = parts[k][base + g * half : base + (g + 1) * half, :].astype(F32)
                    left = jnp.concatenate([both, pltpu.roll(both, 64, 1)], axis=0)
                    base = base + features // 2
                    right = pltpu.roll(parts[k][base:, :].astype(F32), (64 - rest_lanes * g) % 128, 1)
                    x = jnp.where(low, left, right)[:, : own_rows - full * 128]
                up, new = step_of(x, f, mom[source[k], rows, cols].astype(F32))
                uv[k, rows, cols] = up
                nv[k, rows, cols] = new
        pltpu.make_async_copy(uv.at[k], update.at[source[k]], usem.at[k]).start()
        pltpu.make_async_copy(nv.at[k], moment.at[source[k]], nsem.at[k]).start()
    for k in range(n):
        pltpu.make_async_copy(uv.at[k], update.at[source[k]], usem.at[k]).wait()
        pltpu.make_async_copy(nv.at[k], moment.at[source[k]], nsem.at[k]).wait()


def emb_lion(parts, which, factor, mom, prior):
    n = len(which)
    shape = jax.ShapeDtypeStruct(mom.shape, BF16)
    buffers = [pltpu.VMEM((n,) + mom.shape[1:], BF16)] * 2
    extra = () if prior is None else prior
    first = 1 + n + 1
    return pl.pallas_call(
        functools.partial(emb_lion_kernel, tuple(which), prior is not None),
        out_shape=(shape, shape),
        in_specs=[SMEM] + [VMEM] * (n + 1) + [ANY] * len(extra),
        out_specs=(ANY, ANY),
        scratch_shapes=buffers + [pltpu.SemaphoreType.DMA((n,))] * 2,
        input_output_aliases={first: 0, first + 1: 1} if extra else {},
        compiler_params=pltpu.CompilerParams(vmem_limit_bytes=LION_BYTES),
        cost_estimate=pl.CostEstimate(flops=n * 3_000_000, bytes_accessed=n * 2_300_000, transcendentals=0),
    )(factor, *[parts[i] for i in which], mom, *extra)


def emb_send(value, step):
    pairs = [(a * 2 + b, emb_peer(a, b, step, 1)) for a in range(4) for b in range(2)]
    return lax.ppermute(value, DP, pairs)


def on_device(emb_grad, emb_mom, blk_grad, blk_mom, tile_group, clip_rms):
    dp_count = lax.axis_size(DP)
    mp_count = lax.axis_size(MP)
    a, b = lax.axis_index("dp_0"), lax.axis_index("dp_1")
    z, x, c = (lax.axis_index(name) for name in MP)
    dp_index = a * 2 + b
    mp_index = z * 4 + x * 2 + c
    groups = clip_rms.shape[0]
    tile_rows, tile_cols = emb_grad.shape
    own_rows = emb_mom.shape[3]
    matrices, block_rows, block_cols = blk_grad.shape
    owner_rows = blk_mom.shape[2]
    row_blocks = tile_group.shape[1] // dp_count
    block_height = block_rows // row_blocks
    emb_t = emb_grad.T
    packed = pl.pallas_call(
        functools.partial(blk_pack_kernel, groups),
        out_shape=jax.ShapeDtypeStruct((mp_count, BLK_ROWS, 128), BF16),
        in_specs=[SMEM, ANY, ANY],
        out_specs=ANY,
        scratch_shapes=[
            pltpu.VMEM((16, BLK_ROWS, 128), BF16),
            pltpu.VMEM(blk_grad.shape, BF16),
            pltpu.VMEM(emb_t.shape, BF16),
            pltpu.SemaphoreType.DMA((2,)),
            pltpu.SemaphoreType.DMA((7,)),
            pltpu.SemaphoreType.DMA((1,)),
        ],
        compiler_params=pltpu.CompilerParams(vmem_limit_bytes=VMEM_BYTES),
        cost_estimate=pl.CostEstimate(flops=10_000_000, bytes_accessed=9_000_000, transcendentals=0),
        name="blk_pack",
    )(tile_group, blk_grad, emb_t)
    blk_parts = lax.all_to_all(packed, MP, split_axis=0, concat_axis=0, tiled=True)

    emb_payload = jax.ShapeDtypeStruct((EMB_ROWS, 128), BF16)
    emb_packed = pl.pallas_call(
        emb_pack_kernel,
        out_shape=(emb_payload,) * 8,
        in_specs=[ANY],
        out_specs=(ANY,) * 8,
        scratch_shapes=[
            pltpu.VMEM((8, EMB_ROWS, 128), BF16),
            pltpu.VMEM(emb_t.shape, BF16),
            pltpu.SemaphoreType.DMA((7,)),
            pltpu.SemaphoreType.DMA((8,)),
        ],
        compiler_params=pltpu.CompilerParams(vmem_limit_bytes=VMEM_BYTES),
        cost_estimate=pl.CostEstimate(flops=10_000_000, bytes_accessed=9_000_000, transcendentals=0),
        name="emb_pack",
    )(emb_t)
    emb_parts = [emb_send(v, s) for v, s in zip(emb_packed[:7], EMB_STEPS)] + [emb_packed[7]]

    pieces = jnp.sum(blk_parts[:, SUM_ROW, SUM_LANE : SUM_LANE + 3 * groups].astype(F32), axis=0)
    pieces = sum(emb_send(pieces, s) for s in EMB_STEPS[:7]) + pieces
    totals = jnp.sum(pieces.reshape(groups, 3), axis=1)

    labels = jnp.arange(groups, dtype=jnp.int32)
    first = (labels == 0).astype(F32)
    onehot = (tile_group[..., None] == labels).astype(F32)
    counts = jnp.sum(onehot, axis=(0, 1, 2)) * float(block_height * block_cols) + first * float(
        tile_rows * mp_count * tile_cols * dp_count
    )
    root_mean = jnp.sqrt(totals / jnp.maximum(counts, 1.0))
    factor = jnp.minimum(1.0, clip_rms / (root_mean + epsilon))
    owner_block = dp_index * row_blocks + mp_index * owner_rows // block_height
    owner_ids = lax.dynamic_index_in_dim(onehot, owner_block, axis=1, keepdims=False)
    owner_factor = jnp.sum(owner_ids * factor, axis=-1)

    mom_t = jnp.transpose(blk_mom, (0, 2, 1, 3))
    shape = jax.ShapeDtypeStruct(mom_t.shape, BF16)
    blk_update, blk_moment = pl.pallas_call(
        blk_lion_kernel,
        out_shape=(shape, shape),
        in_specs=[SMEM, VMEM, VMEM],
        out_specs=(ANY, ANY),
        scratch_shapes=[
            pltpu.VMEM((block_cols // 128 + 1, matrices * owner_rows * 16, 128), F32),
            pltpu.VMEM(mom_t.shape, BF16),
            pltpu.VMEM(mom_t.shape, BF16),
            pltpu.SemaphoreType.DMA((4,)),
        ],
        compiler_params=pltpu.CompilerParams(vmem_limit_bytes=LION_BYTES),
        cost_estimate=pl.CostEstimate(flops=10_000_000, bytes_accessed=9_000_000, transcendentals=0),
        name="blk_lion",
    )(owner_factor, blk_parts, mom_t)

    emb_mom_t = jnp.transpose(emb_mom.reshape(dp_count, own_rows, tile_cols), (0, 2, 1))
    early = [7, 0, 1, 3, 5, 2]
    late = [4, 6]
    outs = None
    for which in (early, late):
        outs = emb_lion(
            emb_parts,
            which,
            factor[:1],
            emb_mom_t,
            outs,
        )
    emb_update, emb_moment = (jnp.transpose(v, (0, 2, 1)).reshape(emb_mom.shape) for v in outs)
    return (
        emb_update,
        emb_moment,
        jnp.transpose(blk_update, (0, 2, 1, 3)),
        jnp.transpose(blk_moment, (0, 2, 1, 3)),
    )


def solution(mesh):
    torus = Mesh(mesh.devices.reshape(4, 2, 4, 2, 2), DP_MP)
    return jax.shard_map(
        on_device,
        mesh=torus,
        in_specs=(
            P(MP, DP),
            P(MP, None, DP, None, None),
            P(None, DP, MP),
            P(None, None, DP_MP, None),
            P(),
            P(),
        ),
        out_specs=(
            P(MP, None, DP, None, None),
            P(MP, None, DP, None, None),
            P(None, None, DP_MP, None),
            P(None, None, DP_MP, None),
        ),
        check_vma=False,
    )
```

time: 141 us -> 135 us (0.957)
  the two profiles are of different devices: /device:TPU:1 before, /device:TPU:0 now
where the time goes in v1:
time: 135 us; the launch traced here: 134 us
  starting transfers between devices  48.2 us (36%)
  waiting for transfers between devices  48 us (36%)
  Pallas kernels  29.5 us (22%)
  local copies, waits for them, and re-layouts  4.05 us (3%)
  other arithmetic  3.34 us (2%)
    ppermute x14, starting transfers between devices, emb_send(): return lax.ppermute(value, DP, pairs)  41.7 us
    ppermute x14, waiting for transfers between devices, emb_send(): return lax.ppermute(value, DP, pairs)  38.3 us
    all_to_all x1, waiting for transfers between devices, on_device(): lax.all_to_all(packed, MP, split_axis=0, concat_axis=0, tiled=True)  9.76 us
    pallas_call x2, Pallas kernels, emb_lion(): pl.pallas_call(functools.partial(emb_lion_kernel, tuple(which), prior is...  7.94 us
    pallas_call x1, Pallas kernels, on_device(): pl.pallas_call(emb_pack_kernel, out_shape=(emb_payload,) * 8, in_specs=[A...  7.88 us
    pallas_call x1, Pallas kernels, on_device(): pl.pallas_call(blk_lion_kernel, out_shape=(shape, shape), in_specs=[SMEM,...  7.44 us
    all_to_all x1, starting transfers between devices, on_device(): lax.all_to_all(packed, MP, split_axis=0, concat_axis=0, tiled=True)  6.51 us
    pallas_call x1, Pallas kernels, on_device(): pl.pallas_call(functools.partial(blk_pack_kernel, groups), out_shape=jax....  6.26 us
  transfers between devices with their start and end apart: 15, of which 8 were waited for; matrix products, arithmetic and copies ran while one was open for 3% of the time, Pallas kernels for 16%

profile of v1, /device:TPU:0, one launch (start us, length us, event | category | flops | bytes accessed | tf_op | source)
XLA Modules:
  0.0 134.1 jit_solution(7587884824837178196)
XLA Ops:
  0.6 6.3 %blk_pack.1 = bf16[16,520,128]{2,1,0:T(8,128)(2,1)} custom-call(s32[2,16,16]{2,1,0:T(8,128)} %label_ref.1, bf16[2,448,1184]{2,1,0:T(8,128)(2,1)} %grad.1, bf16[448,4752]{1,0:T(8,128)(2,1)} %bitcast.27), custom_call_target="tpu_custom_call" | custom-call | flops 10000000 | bytes 9000000 | tf_op jit(solution)/shard_map/blk_pack/pallas_call | solution.py:307
  6.9 6.5 %all-to-all-start = ((bf16[16,520,128]{2,1,0:T(8,128)(2,1)}), bf16[16,520,128]{2,1,0:T(8,128)(2,1)}, u32[]{:S(2)}, u32[]{:S(2)}) async-start(bf16[16,520,128]{2,1,0:T(8,128)(2,1)} %blk_pack.1), calls=%async_computation | async-start | bytes 4259840 | tf_op jit(solution)/shard_map/all_to_all | solution.py:324
  13.4 7.9 %emb_pack.1 = (bf16[2080,128]{1,0:T(8,128)(2,1)}, bf16[2080,128]{1,0:T(8,128)(2,1)}, bf16[2080,128]{1,0:T(8,128)(2,1)}, bf16[2080,128]{1,0:T(8,128)(2,1)}, bf16[...) custom-call(bf16[448,4752]{1,0:T(8,128)(2,1)} %bitcast.28), custom_call_target="tpu_custom_call" | custom-call | flops 10000000 | bytes 9000000 | tf_op jit(solution)/shard_map/emb_pack/pallas_call | solution.py:327
  21.3 1.6 %collective-permute-start.10 = (bf16[2080,128]{1,0:T(8,128)(2,1)}, bf16[2080,128]{1,0:T(8,128)(2,1)S(1)}, u32[]{:S(2)}, u32[]{:S(2)}) collective-permute-start(bf16[2080,128]{1,0:T(8,128)(2,1)} %get-tuple-element.22), channel_id=1, source_target_pairs={{0,32},{16,48},{32,64},{48,80},{64,96},{80,112},{96,0},{112,16},{1... | collective-permute-start | bytes 1597448 | tf_op jit(solution)/shard_map/ppermute | solution.py:289
  23.0 2.9 %collective-permute-start.11 = (bf16[2080,128]{1,0:T(8,128)(2,1)}, bf16[2080,128]{1,0:T(8,128)(2,1)S(1)}, u32[]{:S(2)}, u32[]{:S(2)}) collective-permute-start(bf16[2080,128]{1,0:T(8,128)(2,1)} %get-tuple-element.23), channel_id=1, source_target_pairs={{0,64},{16,80},{32,96},{48,112},{64,0},{80,16},{96,32},{112,48},{1... | collective-permute-start | bytes 1597448 | tf_op jit(solution)/shard_map/ppermute | solution.py:289
  25.9 1.3 %collective-permute-start.12 = (bf16[2080,128]{1,0:T(8,128)(2,1)}, bf16[2080,128]{1,0:T(8,128)(2,1)S(1)}, u32[]{:S(2)}, u32[]{:S(2)}) collective-permute-start(bf16[2080,128]{1,0:T(8,128)(2,1)} %get-tuple-element.24), channel_id=1, source_target_pairs={{0,96},{16,112},{32,0},{48,16},{64,32},{80,48},{96,64},{112,80},{1... | collective-permute-start | bytes 1597448 | tf_op jit(solution)/shard_map/ppermute | solution.py:289
  27.2 2.8 %collective-permute-start.13 = (bf16[2080,128]{1,0:T(8,128)(2,1)}, bf16[2080,128]{1,0:T(8,128)(2,1)S(1)}, u32[]{:S(2)}, u32[]{:S(2)}) collective-permute-start(bf16[2080,128]{1,0:T(8,128)(2,1)} %get-tuple-element.25), channel_id=1, source_target_pairs={{0,48},{16,32},{32,80},{48,64},{64,112},{80,96},{96,16},{112,0},{1... | collective-permute-start | bytes 1597448 | tf_op jit(solution)/shard_map/ppermute | solution.py:289
  30.1 0.8 collective-permute-start.9
  30.9 0.9 fusion.1
  31.7 0.7 fusion
  32.5 9.8 %all-to-all-done.rest_0_ = bf16[16,520,128]{2,1,0:T(8,128)(2,1)} async-done(((bf16[16,520,128]{2,1,0:T(8,128)(2,1)}), bf16[16,520,128]{2,1,0:T(8,128)(2,1)}, u32[]{:S(2)}, u32[]{:S(2)}) %all-to-all-start) | async-done | bytes 2129952 | tf_op jit(solution)/shard_map/all_to_all | solution.py:324
  42.2 0.9 fusion.2
  43.1 0.0 collective-permute-done.10.rest_2_
  43.1 21.1 %collective-permute-start.7 = (bf16[2080,128]{1,0:T(8,128)(2,1)}, bf16[2080,128]{1,0:T(8,128)(2,1)S(1)}, u32[]{:S(2)}, u32[]{:S(2)}) collective-permute-start(bf16[2080,128]{1,0:T(8,128)(2,1)} %get-tuple-element.18), channel_id=1, source_target_pairs={{0,80},{16,64},{32,112},{48,96},{64,16},{80,0},{96,48},{112,32},{1... | collective-permute-start | bytes 1597448 | tf_op jit(solution)/shard_map/ppermute | solution.py:289
  64.1 0.0 collective-permute-done.11.rest_3_
  64.1 0.8 collective-permute-start
  64.9 11.1 %collective-permute-done = f32[12]{0:T(128)S(1)} collective-permute-done((f32[12]{0:T(128)S(1)}, f32[12]{0:T(128)S(1)}, u32[]{:S(2)}, u32[]{:S(2)}) %collective-permute-start) | collective-permute-done | bytes 80 | tf_op jit(solution)/shard_map/ppermute | solution.py:289
  76.0 1.5 %collective-permute-start.1 = (f32[12]{0:T(128)S(1)}, f32[12]{0:T(128)S(1)}, u32[]{:S(2)}, u32[]{:S(2)}) collective-permute-start(f32[12]{0:T(128)S(1)} %fusion.2), channel_id=1, source_target_pairs={{0,32},{16,48},{32,64},{48,80},{64,96},{80,112},{96,0},{112,16},{1... | collective-permute-start | bytes 152 | tf_op jit(solution)/shard_map/ppermute | solution.py:289
  77.6 3.2 %collective-permute-done.1 = f32[12]{0:T(128)S(1)} collective-permute-done((f32[12]{0:T(128)S(1)}, f32[12]{0:T(128)S(1)}, u32[]{:S(2)}, u32[]{:S(2)}) %collective-permute-start.1) | collective-permute-done | bytes 80 | tf_op jit(solution)/shard_map/ppermute | solution.py:289
  80.8 0.6 collective-permute-start.2
  81.4 6.6 %collective-permute-done.2 = f32[12]{0:T(128)S(1)} collective-permute-done((f32[12]{0:T(128)S(1)}, f32[12]{0:T(128)S(1)}, u32[]{:S(2)}, u32[]{:S(2)}) %collective-permute-start.2) | collective-permute-done | bytes 80 | tf_op jit(solution)/shard_map/ppermute | solution.py:289
  88.0 0.8 collective-permute-start.3
  88.8 4.3 %collective-permute-done.3 = f32[12]{0:T(128)S(1)} collective-permute-done((f32[12]{0:T(128)S(1)}, f32[12]{0:T(128)S(1)}, u32[]{:S(2)}, u32[]{:S(2)}) %collective-permute-start.3) | collective-permute-done | bytes 80 | tf_op jit(solution)/shard_map/ppermute | solution.py:289
  93.1 1.0 collective-permute-start.4
  94.1 6.5 %collective-permute-done.4 = f32[12]{0:T(128)S(1)} collective-permute-done((f32[12]{0:T(128)S(1)}, f32[12]{0:T(128)S(1)}, u32[]{:S(2)}, u32[]{:S(2)}) %collective-permute-start.4) | collective-permute-done | bytes 80 | tf_op jit(solution)/shard_map/ppermute | solution.py:289
  100.6 0.8 collective-permute-start.5
  101.3 2.8 %collective-permute-done.5 = f32[12]{0:T(128)S(1)} collective-permute-done((f32[12]{0:T(128)S(1)}, f32[12]{0:T(128)S(1)}, u32[]{:S(2)}, u32[]{:S(2)}) %collective-permute-start.5) | collective-permute-done | bytes 80 | tf_op jit(solution)/shard_map/ppermute | solution.py:289
  104.1 2.2 %collective-permute-start.6 = (f32[12]{0:T(128)S(1)}, f32[12]{0:T(128)S(1)}, u32[]{:S(2)}, u32[]{:S(2)}) collective-permute-start(f32[12]{0:T(128)S(1)} %fusion.2), channel_id=1, source_target_pairs={{0,112},{16,96},{32,16},{48,0},{64,48},{80,32},{96,80},{112,64},{1... | collective-permute-start | bytes 152 | tf_op jit(solution)/shard_map/ppermute | solution.py:289
  106.4 3.8 %collective-permute-done.6 = f32[12]{0:T(128)S(1)} collective-permute-done((f32[12]{0:T(128)S(1)}, f32[12]{0:T(128)S(1)}, u32[]{:S(2)}, u32[]{:S(2)}) %collective-permute-start.6) | collective-permute-done | bytes 80 | tf_op jit(solution)/shard_map/ppermute | solution.py:289
  110.1 3.4 %collective-permute-start.8 = (bf16[2080,128]{1,0:T(8,128)(2,1)}, bf16[2080,128]{1,0:T(8,128)(2,1)S(1)}, u32[]{:S(2)}, u32[]{:S(2)}) collective-permute-start(bf16[2080,128]{1,0:T(8,128)(2,1)} %get-tuple-element.19), channel_id=1, source_target_pairs={{0,112},{16,96},{32,16},{48,0},{64,48},{80,32},{96,80},{112,64},{1... | collective-permute-start | bytes 1597448 | tf_op jit(solution)/shard_map/ppermute | solution.py:289
  113.6 0.1 reshape.23
  113.6 0.1 reduce_sum.37
  113.8 0.7 fusion.5
  114.4 0.1 fusion.3.factor_ref
  114.5 0.0 copy-start.2
  114.5 1.7 %copy-done.2 = bf16[2,16,28,1184]{3,1,2,0:T(8,128)(2,1)S(1)} copy-done((bf16[2,16,28,1184]{3,1,2,0:T(8,128)(2,1)S(1)}, bf16[2,16,28,1184]{3,1,2,0:T(8,128)(2,1)}, u32[]{:S(2)}) %copy-start.2) | copy-done | bytes 2121752
  116.2 7.4 %blk_lion.1 = (bf16[2,28,16,1184]{3,2,1,0:T(8,128)(2,1)}, bf16[2,28,16,1184]{3,2,1,0:T(8,128)(2,1)}) custom-call(f32[2,16]{1,0:T(2,128)S(1)} %fusion.3.factor_ref, bf16[16,520,128]{2,1,0:T(8,128)(2,1)} %all-to-all-done.rest_0_, bf16[2,28,16,1184]{3,2,1,0:T(8,128)(2,1)S(1)} %bitcast.24), custom_call_target="tpu_custom_call" | custom-call | flops 10000000 | bytes 9000000 | tf_op jit(solution)/shard_map/blk_lion/pallas_call | solution.py:362
  123.6 0.0 collective-permute-done.12.rest_4_
  123.6 0.0 collective-permute-done.13.rest_5_
  123.7 0.0 collective-permute-done.9.rest_1_
  123.7 0.0 copy-done.3
  123.7 0.0 copy-start
  123.7 2.3 %copy-done = bf16[1,8,1,594,448]{3,4,2,1,0:T(8,128)(2,1)S(1)} copy-done((bf16[1,8,1,594,448]{3,4,2,1,0:T(8,128)(2,1)S(1)}, bf16[1,8,1,594,448]{3,4,2,1,0:T(8,128)(2,1)}, u32[]{:S(2)}) %copy-start) | copy-done | bytes 4257816
  126.0 5.7 %shard_map.93 = (bf16[8,448,594]{2,1,0:T(8,128)(2,1)}, bf16[8,448,594]{2,1,0:T(8,128)(2,1)}) custom-call(f32[1]{0:T(128)S(1)} %bitcast.25, bf16[2080,128]{1,0:T(8,128)(2,1)S(1)} %copy-done.3, bf16[2080,128]{1,0:T(8,128)(2,1)} %collective-permute-done.9.rest_1_, bf16[2080,128]{1,0:T(8,128)(2,1)S(1)} %collective-permute-done.10.rest_2_, ...), custom_call_target="tpu_custom_call" | custom-call | flops 18000000 | bytes 13800000 | tf_op jit(solution)/shard_map/pallas_call | solution.py:275
  131.7 0.0 collective-permute-done.7.rest_0_
  131.7 0.0 collective-permute-done.8.rest_1_
  131.7 0.0 copy-done.1
  131.7 2.2 %shard_map.94 = (bf16[8,448,594]{2,1,0:T(8,128)(2,1)}, bf16[8,448,594]{2,1,0:T(8,128)(2,1)}) custom-call(f32[1]{0:T(128)S(1)} %bitcast.26, bf16[2080,128]{1,0:T(8,128)(2,1)S(1)} %collective-permute-done.7.rest_0_, bf16[2080,128]{1,0:T(8,128)(2,1)S(1)} %collective-permute-done.8.rest_1_, ...), custom_call_target="tpu_custom_call", output_to_operand_aliasing={{0}: (4, {}), {1}: (5, {})} | custom-call | flops 6000000 | bytes 4600000 | tf_op jit(solution)/shard_map/pallas_call | solution.py:275
  (3 shorter events, 0.0 us)
Async XLA Ops:
  6.9 35.3 %all-to-all-start = ((bf16[16,520,128]{2,1,0:T(8,128)(2,1)}), bf16[16,520,128]{2,1,0:T(8,128)(2,1)}, u32[]{:S(2)}, u32[]{:S(2)}) async-start(bf16[16,520,128]{2,1,0:T(8,128)(2,1)} %blk_pack.1), calls=%async_computation | async-start | bytes 4259840 | tf_op jit(solution)/shard_map/all_to_all | solution.py:324
  21.3 21.8 %collective-permute-start.10 = (bf16[2080,128]{1,0:T(8,128)(2,1)}, bf16[2080,128]{1,0:T(8,128)(2,1)S(1)}, u32[]{:S(2)}, u32[]{:S(2)}) collective-permute-start(bf16[2080,128]{1,0:T(8,128)(2,1)} %get-tuple-element.22), channel_id=1, source_target_pairs={{0,32},{16,48},{32,64},{48,80},{64,96},{80,112},{96,0},{112,16},{1... | collective-permute-start | bytes 1597448 | tf_op jit(solution)/shard_map/ppermute | solution.py:289
  23.0 41.2 %collective-permute-start.11 = (bf16[2080,128]{1,0:T(8,128)(2,1)}, bf16[2080,128]{1,0:T(8,128)(2,1)S(1)}, u32[]{:S(2)}, u32[]{:S(2)}) collective-permute-start(bf16[2080,128]{1,0:T(8,128)(2,1)} %get-tuple-element.23), channel_id=1, source_target_pairs={{0,64},{16,80},{32,96},{48,112},{64,0},{80,16},{96,32},{112,48},{1... | collective-permute-start | bytes 1597448 | tf_op jit(solution)/shard_map/ppermute | solution.py:289
  25.9 97.8 %collective-permute-start.12 = (bf16[2080,128]{1,0:T(8,128)(2,1)}, bf16[2080,128]{1,0:T(8,128)(2,1)S(1)}, u32[]{:S(2)}, u32[]{:S(2)}) collective-permute-start(bf16[2080,128]{1,0:T(8,128)(2,1)} %get-tuple-element.24), channel_id=1, source_target_pairs={{0,96},{16,112},{32,0},{48,16},{64,32},{80,48},{96,64},{112,80},{1... | collective-permute-start | bytes 1597448 | tf_op jit(solution)/shard_map/ppermute | solution.py:289
  27.2 96.4 %collective-permute-start.13 = (bf16[2080,128]{1,0:T(8,128)(2,1)}, bf16[2080,128]{1,0:T(8,128)(2,1)S(1)}, u32[]{:S(2)}, u32[]{:S(2)}) collective-permute-start(bf16[2080,128]{1,0:T(8,128)(2,1)} %get-tuple-element.25), channel_id=1, source_target_pairs={{0,48},{16,32},{32,80},{48,64},{64,112},{80,96},{96,16},{112,0},{1... | collective-permute-start | bytes 1597448 | tf_op jit(solution)/shard_map/ppermute | solution.py:289
  30.1 93.6 %collective-permute-start.9 = (bf16[2080,128]{1,0:T(8,128)(2,1)}, bf16[2080,128]{1,0:T(8,128)(2,1)}, u32[]{:S(2)}, u32[]{:S(2)}) collective-permute-start(bf16[2080,128]{1,0:T(8,128)(2,1)} %get-tuple-element.21), channel_id=1, source_target_pairs={{0,16},{16,0},{32,48},{48,32},{64,80},{80,64},{96,112},{112,96},{1... | collective-permute-start | bytes 1597448 | tf_op jit(solution)/shard_map/ppermute | solution.py:289
  43.1 88.6 %collective-permute-start.7 = (bf16[2080,128]{1,0:T(8,128)(2,1)}, bf16[2080,128]{1,0:T(8,128)(2,1)S(1)}, u32[]{:S(2)}, u32[]{:S(2)}) collective-permute-start(bf16[2080,128]{1,0:T(8,128)(2,1)} %get-tuple-element.18), channel_id=1, source_target_pairs={{0,80},{16,64},{32,112},{48,96},{64,16},{80,0},{96,48},{112,32},{1... | collective-permute-start | bytes 1597448 | tf_op jit(solution)/shard_map/ppermute | solution.py:289
  64.1 11.9 %collective-permute-start = (f32[12]{0:T(128)S(1)}, f32[12]{0:T(128)S(1)}, u32[]{:S(2)}, u32[]{:S(2)}) collective-permute-start(f32[12]{0:T(128)S(1)} %fusion.2), channel_id=1, source_target_pairs={{0,16},{16,0},{32,48},{48,32},{64,80},{80,64},{96,112},{112,96},{1... | collective-permute-start | bytes 152 | tf_op jit(solution)/shard_map/ppermute | solution.py:289
  76.0 4.8 %collective-permute-start.1 = (f32[12]{0:T(128)S(1)}, f32[12]{0:T(128)S(1)}, u32[]{:S(2)}, u32[]{:S(2)}) collective-permute-start(f32[12]{0:T(128)S(1)} %fusion.2), channel_id=1, source_target_pairs={{0,32},{16,48},{32,64},{48,80},{64,96},{80,112},{96,0},{112,16},{1... | collective-permute-start | bytes 152 | tf_op jit(solution)/shard_map/ppermute | solution.py:289
  80.8 7.2 %collective-permute-start.2 = (f32[12]{0:T(128)S(1)}, f32[12]{0:T(128)S(1)}, u32[]{:S(2)}, u32[]{:S(2)}) collective-permute-start(f32[12]{0:T(128)S(1)} %fusion.2), channel_id=1, source_target_pairs={{0,48},{16,32},{32,80},{48,64},{64,112},{80,96},{96,16},{112,0},{1... | collective-permute-start | bytes 152 | tf_op jit(solution)/shard_map/ppermute | solution.py:289
  88.0 5.1 %collective-permute-start.3 = (f32[12]{0:T(128)S(1)}, f32[12]{0:T(128)S(1)}, u32[]{:S(2)}, u32[]{:S(2)}) collective-permute-start(f32[12]{0:T(128)S(1)} %fusion.2), channel_id=1, source_target_pairs={{0,64},{16,80},{32,96},{48,112},{64,0},{80,16},{96,32},{112,48},{1... | collective-permute-start | bytes 152 | tf_op jit(solution)/shard_map/ppermute | solution.py:289
  93.1 7.5 %collective-permute-start.4 = (f32[12]{0:T(128)S(1)}, f32[12]{0:T(128)S(1)}, u32[]{:S(2)}, u32[]{:S(2)}) collective-permute-start(f32[12]{0:T(128)S(1)} %fusion.2), channel_id=1, source_target_pairs={{0,80},{16,64},{32,112},{48,96},{64,16},{80,0},{96,48},{112,32},{1... | collective-permute-start | bytes 152 | tf_op jit(solution)/shard_map/ppermute | solution.py:289
  100.6 3.6 %collective-permute-start.5 = (f32[12]{0:T(128)S(1)}, f32[12]{0:T(128)S(1)}, u32[]{:S(2)}, u32[]{:S(2)}) collective-permute-start(f32[12]{0:T(128)S(1)} %fusion.2), channel_id=1, source_target_pairs={{0,96},{16,112},{32,0},{48,16},{64,32},{80,48},{96,64},{112,80},{1... | collective-permute-start | bytes 152 | tf_op jit(solution)/shard_map/ppermute | solution.py:289
  104.1 6.0 %collective-permute-start.6 = (f32[12]{0:T(128)S(1)}, f32[12]{0:T(128)S(1)}, u32[]{:S(2)}, u32[]{:S(2)}) collective-permute-start(f32[12]{0:T(128)S(1)} %fusion.2), channel_id=1, source_target_pairs={{0,112},{16,96},{32,16},{48,0},{64,48},{80,32},{96,80},{112,64},{1... | collective-permute-start | bytes 152 | tf_op jit(solution)/shard_map/ppermute | solution.py:289
  110.1 21.6 %collective-permute-start.8 = (bf16[2080,128]{1,0:T(8,128)(2,1)}, bf16[2080,128]{1,0:T(8,128)(2,1)S(1)}, u32[]{:S(2)}, u32[]{:S(2)}) collective-permute-start(bf16[2080,128]{1,0:T(8,128)(2,1)} %get-tuple-element.19), channel_id=1, source_target_pairs={{0,112},{16,96},{32,16},{48,0},{64,48},{80,32},{96,80},{112,64},{1... | collective-permute-start | bytes 1597448 | tf_op jit(solution)/shard_map/ppermute | solution.py:289
  114.5 1.7 %copy-start.2 = (bf16[2,16,28,1184]{3,1,2,0:T(8,128)(2,1)S(1)}, bf16[2,16,28,1184]{3,1,2,0:T(8,128)(2,1)}, u32[]{:S(2)}) copy-start(bf16[2,16,28,1184]{3,1,2,0:T(8,128)(2,1)} %param.9) | copy-start | bytes 6365188
  116.2 7.5 %copy-start.3 = (bf16[2080,128]{1,0:T(8,128)(2,1)S(1)}, bf16[2080,128]{1,0:T(8,128)(2,1)}, u32[]{:S(2)}) copy-start(bf16[2080,128]{1,0:T(8,128)(2,1)} %get-tuple-element.20.rest_0_) | copy-start | bytes 1597444
  123.7 2.3 %copy-start = (bf16[1,8,1,594,448]{3,4,2,1,0:T(8,128)(2,1)S(1)}, bf16[1,8,1,594,448]{3,4,2,1,0:T(8,128)(2,1)}, u32[]{:S(2)}) copy-start(bf16[1,8,1,594,448]{3,4,2,1,0:T(8,128)(2,1)} %param.7) | copy-start | bytes 12773380
  126.0 5.7 %copy-start.1 = (bf16[1,8,1,594,448]{3,4,2,1,0:T(8,128)(2,1)S(1)}, bf16[1,8,1,594,448]{3,4,2,1,0:T(8,128)(2,1)}, u32[]{:S(2)}) copy-start(bf16[1,8,1,594,448]{3,4,2,1,0:T(8,128)(2,1)} %param.7) | copy-start | bytes 12773380

commit v2 on v1

v2 whole, which is shorter than its diff:
```python
import functools

import jax
import jax.numpy as jnp
from jax import lax
from jax.experimental import pallas as pl
from jax.experimental.pallas import tpu as pltpu
from jax.sharding import Mesh
from jax.sharding import PartitionSpec as P


DP = ("dp_0", "dp_1")
MP = ("mp_0", "mp_1", "mp_2")
DP_MP = DP + MP


beta_first = 0.9
beta_second = 0.99
temper = 0.05
epsilon = 1e-06

VMEM_BYTES = 67_043_328
F32 = jnp.float32
BF16 = jnp.bfloat16
ANY = pl.BlockSpec(memory_space=pltpu.HBM)
VMEM = pl.BlockSpec(memory_space=pltpu.VMEM)
SMEM = pl.BlockSpec(memory_space=pltpu.SMEM)

EMB_ROWS = 2080
BLK_ROWS = 520
SUM_ROW = 512
SUM_LANE = 96


EMB_STEPS = [(0, 1), (1, 0), (1, 1), (2, 0), (2, 1), (3, 0), (3, 1), (0, 0)]


def emb_peer(a, b, step, sign):
    return ((a + sign * step[0] + 4) % 4) * 2 + (b ^ step[1])


def lanes(shape):
    return lax.broadcasted_iota(jnp.int32, shape, len(shape) - 1)


def split_three(value):
    high = value.astype(BF16).astype(F32)
    middle = (value - high).astype(BF16).astype(F32)
    low = (value - high - middle).astype(BF16).astype(F32)
    return high, middle, low


def fold8(x):
    return jnp.sum(x.reshape(x.shape[0] // 8, 8, x.shape[1]), axis=0)


def emb_peers(sign):
    a, b = (lax.axis_index(name) for name in DP)
    return [emb_peer(a, b, step, sign) for step in EMB_STEPS]


def blk_pack_kernel(groups, label_ref, grad, emb, *rest):
    dp_index = lax.axis_index("dp_0") * 2 + lax.axis_index("dp_1")
    mp_index = lax.axis_index("mp_0") * 4 + lax.axis_index("mp_1") * 2 + lax.axis_index("mp_2")
    out, stage, ending, xb, xe, bsem, esem, osem = rest
    matrices, block_rows, block_cols = xb.shape
    count = stage.shape[0]
    owner_rows = block_rows // count
    half = block_rows // 2
    step = 64
    steps = xe.shape[0] // step
    for m in range(matrices):
        pltpu.make_async_copy(grad.at[m], xb.at[m], bsem.at[m]).start()
    for g in range(steps):
        pltpu.make_async_copy(
            emb.at[pl.ds(g * step, step)], xe.at[pl.ds(g * step, step)], esem.at[g]
        ).start()
    full = block_cols // 128
    for m in range(matrices):
        pltpu.make_async_copy(grad.at[m], xb.at[m], bsem.at[m]).wait()
    block_sums = []
    for m in range(matrices):
        for h in range(2):
            x = xb[m, h * half : (h + 1) * half, :].astype(F32)
            block_sums.append(jnp.sum(fold8(x * x)))
    for j in range(count):
        x = jnp.concatenate(
            [xb[m, j * owner_rows : (j + 1) * owner_rows, :].astype(F32) for m in range(matrices)],
            axis=0,
        )
        rows = x.shape[0]
        for t in range(full):
            stage[j, t * rows : (t + 1) * rows, :] = x[:, t * 128 : (t + 1) * 128].astype(BF16)
        tail = x[:, full * 128 :]
        for q in range(4):
            base = rows * full
            stage[j, base : base + 8, q * 32 : (q + 1) * 32] = tail[q * 16 : q * 16 + 8, :].astype(BF16)
            if q < 3:
                ending[j, :, q * 32 : (q + 1) * 32] = tail[q * 16 + 8 : q * 16 + 16, :].astype(BF16)
    main = pltpu.make_async_copy(stage, out.at[:, pl.ds(0, SUM_ROW)], osem.at[0])
    main.start()
    acc = jnp.zeros((8, 512), F32)
    tail_acc = jnp.zeros((8, xe.shape[1] % 512), F32)
    for g in range(steps):
        pltpu.make_async_copy(
            emb.at[pl.ds(g * step, step)], xe.at[pl.ds(g * step, step)], esem.at[g]
        ).wait()
        for c in range(xe.shape[1] // 512):
            x = xe[g * step : (g + 1) * step, c * 512 : (c + 1) * 512].astype(F32)
            acc = acc + fold8(x * x)
        x = xe[g * step : (g + 1) * step, xe.shape[1] // 512 * 512 :].astype(F32)
        tail_acc = tail_acc + fold8(x * x)
    emb_sum = jnp.sum(acc) + jnp.sum(tail_acc)
    lane = lanes((8, 128))
    sums = jnp.zeros((8, 128), F32)
    for g in range(groups):
        total = emb_sum if g == 0 else jnp.float32(0)
        for i, s in enumerate(block_sums):
            label = label_ref[i // 2, dp_index * 2 + i % 2, mp_index]
            total = total + jnp.where(label == g, s, jnp.float32(0))
        for p, piece in enumerate(split_three(jnp.full((8, 128), total, F32))):
            sums = jnp.where(lane == SUM_LANE + 3 * g + p, piece, sums)
    for j in range(count):
        ending[j] = jnp.where(lane < SUM_LANE, ending[j].astype(F32), sums).astype(BF16)
    last = pltpu.make_async_copy(ending, out.at[:, pl.ds(SUM_ROW, 8)], osem.at[1])
    last.start()
    main.wait()
    last.wait()


def emb_pack_rows(tile, write, features, own_rows, d, g, step):
    full = own_rows // 128
    rest_lanes = own_rows - full * 128 - 64
    lane = lanes((step, 128))
    low = lanes((step // 2, 128)) < 64
    q, r = divmod(d * own_rows, 128)
    need = -(-(r + own_rows) // 128)
    turned = [pltpu.roll(tile(q + i), 128 - r, 1) if r else tile(q + i) for i in range(need)]
    for t in range(full + 1):
        x = turned[t]
        if r and t + 1 < need:
            x = jnp.where(lane < 128 - r, x, turned[t + 1])
        if t < full:
            write[t * features + g * step : t * features + (g + 1) * step, :] = x.astype(BF16)
    half = step // 2
    both = jnp.where(low, x[:half], pltpu.roll(x[half:], 64, 1))
    base = full * features
    write[base + g * half : base + (g + 1) * half, :] = both.astype(BF16)
    base = base + features // 2
    moved = pltpu.roll(x, (rest_lanes * g + 64) % 128, 1)
    if g:
        old = write[base:, :].astype(F32)
        moved = jnp.where(lane < rest_lanes * g, old, moved)
    write[base:, :] = moved.astype(BF16)


def tile_of(ref, g, step, i, first, limit):
    start = (i - first) * 128
    x = ref[g * step : (g + 1) * step, start : min(start + 128, limit)].astype(F32)
    if x.shape[1] < 128:
        x = jnp.concatenate([x, jnp.zeros((step, 128 - x.shape[1]), F32)], axis=1)
    return x


def emb_first_kernel(own_rows, emb, *rest):
    n = len(FIRST)
    outs, (stage, xe, esem, osem) = rest[:n], rest[n:]
    dest = emb_peers(1)
    features, tile_rows = emb.shape
    step = 64
    copies = [
        pltpu.make_async_copy(emb.at[pl.ds(g * step, step)], xe.at[pl.ds(g * step, step)], esem.at[g])
        for g in range(features // step)
    ]
    for c in copies:
        c.start()
    for g in range(features // step):
        copies[g].wait()
        tile = functools.partial(tile_of, xe, g, step, first=0, limit=tile_rows)
        for d in range(tile_rows // own_rows):
            for k, i in enumerate(FIRST):

                @pl.when(dest[i] == d)
                def _():
                    emb_pack_rows(tile, stage.at[k], features, own_rows, d, g, step)

    copies = [pltpu.make_async_copy(stage.at[k], out, osem.at[k]) for k, out in enumerate(outs)]
    for c in copies:
        c.start()
    for c in copies:
        c.wait()


def emb_pack_kernel(emb, *rest):
    outs, (stage, xe, esem, osem) = rest[: len(REST)], rest[len(REST) :]
    dest = emb_peers(1)
    features, tile_rows = xe.shape
    count = stage.shape[0]
    step = 64
    copies = [
        pltpu.make_async_copy(emb.at[pl.ds(g * step, step)], xe.at[pl.ds(g * step, step)], esem.at[g])
        for g in range(features // step)
    ]
    for c in copies:
        c.start()
    for g in range(features // step):
        copies[g].wait()
        tile = functools.partial(tile_of, xe, g, step, first=0, limit=tile_rows)
        for d in range(count):
            emb_pack_rows(tile, stage.at[d], features, tile_rows // count, d, g, step)
    copies = [
        pltpu.make_async_copy(stage.at[dest[i]], out, osem.at[k]) for k, (i, out) in enumerate(zip(REST, outs))
    ]
    for c in copies:
        c.start()
    for c in copies:
        c.wait()


def step_of(grad, factor, moment):
    clipped = grad * factor
    update = jnp.tanh((beta_first * moment + (1.0 - beta_first) * clipped) / temper)
    return update.astype(BF16), (beta_second * moment + (1.0 - beta_second) * clipped).astype(BF16)


def mix_kernel(parts, out, stage, wide, mixed, psem, osem):
    count, _, _ = stage.shape
    matrices, owner_rows, _, block_cols = mixed.shape
    rows = matrices * owner_rows
    full = block_cols // 128
    copy = pltpu.make_async_copy(parts, stage, psem)
    copy.start()
    copy.wait()
    for s in range(count):
        for m in range(matrices):
            place = pl.ds(m * owner_rows * count + s, owner_rows, stride=count)
            for t in range(full):
                x = stage[s, t * rows + m * owner_rows : t * rows + (m + 1) * owner_rows, :]
                wide[t, place, :] = x.astype(F32)
        tail = []
        for q in range(4):
            n = min(16, rows - q * 16)
            x = stage[s, rows * full : rows * full + 16, :].astype(F32)
            tail.append((pltpu.roll(x, 128 - 32 * q, 1) if q else x)[:n])
        tail = jnp.concatenate(tail, axis=0)
        for m in range(matrices):
            place = pl.ds(m * owner_rows * count + s, owner_rows, stride=count)
            wide[full, place, :] = tail[m * owner_rows : (m + 1) * owner_rows]
    for m in range(matrices):
        for r in range(owner_rows):
            base = (m * owner_rows + r) * count
            for t in range(full + 1):
                cols = slice(t * 128, min(t * 128 + 128, block_cols))
                x = wide[t, base : base + count, : cols.stop - cols.start]
                mixed[m, r, :, cols] = x.astype(BF16)
    copy = pltpu.make_async_copy(mixed, out, osem)
    copy.start()
    copy.wait()


def emb_lion_chunk(part, mom, up, new, f):
    features, own_rows = up.shape
    step = 64
    f = jnp.concatenate([f] * (step // 8), axis=0)
    full = own_rows // 128
    rest_lanes = own_rows - full * 128 - 64
    low = lanes((step, 128)) < 64
    for g in range(features // step):
        rows = slice(g * step, (g + 1) * step)
        for t in range(full + 1):
            cols = slice(t * 128, min(t * 128 + 128, own_rows))
            if t < full:
                x = part[t * features + g * step : t * features + (g + 1) * step, :].astype(F32)
            else:
                half = step // 2
                base = full * features
                both = part[base + g * half : base + (g + 1) * half, :].astype(F32)
                left = jnp.concatenate([both, pltpu.roll(both, 64, 1)], axis=0)
                base = base + features // 2
                right = pltpu.roll(part[base:, :].astype(F32), (64 - rest_lanes * g) % 128, 1)
                x = jnp.where(low, left, right)[:, : own_rows - full * 128]
            up[rows, cols], new[rows, cols] = step_of(
                x, f[:, : cols.stop - cols.start], mom[rows, cols].astype(F32)
            )


def group_factor(g, shares_ref, counts_ref, clip_ref):
    total = jnp.float32(0)
    for p in range(3):
        piece = shares_ref[0, 3 * g + p]
        for d in range(1, shares_ref.shape[0]):
            piece = piece + shares_ref[d, 3 * g + p]
        total = total + piece
    total, count, clip = (jnp.full((8, 128), v, F32) for v in (total, counts_ref[g], clip_ref[g]))
    root_mean = jnp.sqrt(total / jnp.maximum(count, 1.0))
    return jnp.minimum(1.0, clip / (root_mean + epsilon))


def lion_kernel(which, shares_ref, counts_ref, clip_ref, label_ref, mixed, blk_mom, emb_mom, *rest):
    n = len(which)
    parts, rest = rest[:n], rest[n:]
    emb_up, emb_new, blk_up, blk_new, gv, bv, pv, ev, eu, en, bu, bn, isem, osem = rest
    source = [emb_peers(-1)[i] for i in which]
    matrices, owner_rows, count, block_cols = blk_mom.shape
    copy = pltpu.make_async_copy
    loads, stores = [], []
    for m in range(matrices):
        loads.append([(mixed.at[m], gv.at[m]), (blk_mom.at[m], bv.at[m])])
        stores.append([(bu.at[m], blk_up.at[m]), (bn.at[m], blk_new.at[m])])
    for k in range(n):
        loads.append([(parts[k], pv.at[k]), (emb_mom.at[source[k]], ev.at[k])])
        stores.append([(eu.at[k], emb_up.at[source[k]]), (en.at[k], emb_new.at[source[k]])])
    loads = [[copy(*c, isem.at[2 * i + j]) for j, c in enumerate(cs)] for i, cs in enumerate(loads)]
    stores = [[copy(*c, osem.at[2 * i + j]) for j, c in enumerate(cs)] for i, cs in enumerate(stores)]
    ahead = 3
    for cs in loads[:ahead]:
        for c in cs:
            c.start()
    factors = [group_factor(g, shares_ref, counts_ref, clip_ref) for g in range(clip_ref.shape[0])]
    row_blocks = label_ref.shape[1]
    dp_index = lax.axis_index("dp_0") * 2 + lax.axis_index("dp_1")
    mp_index = lax.axis_index("mp_0") * 4 + lax.axis_index("mp_1") * 2 + lax.axis_index("mp_2")
    per_dp = row_blocks // 8
    owner_block = dp_index * per_dp + mp_index * per_dp // count
    sublane = lax.broadcasted_iota(jnp.int32, (count, 128), 0)
    for i, cs in enumerate(loads):
        for c in cs:
            c.wait()
        for c in loads[i + ahead] if i + ahead < len(loads) else []:
            c.start()
        if i < matrices:
            f = jnp.zeros((count, 128), F32)
            for s in range(count):
                label = label_ref[i, owner_block, s]
                own = factors[0]
                for g in range(1, len(factors)):
                    own = jnp.where(label == g, factors[g], own)
                f = jnp.where(sublane == s, jnp.concatenate([own] * (count // 8), axis=0), f)
            for r in range(owner_rows):
                for t in range(block_cols // 128 + 1):
                    cols = slice(t * 128, min(t * 128 + 128, block_cols))
                    bu[i, r, :, cols], bn[i, r, :, cols] = step_of(
                        gv[i, r, :, cols].astype(F32),
                        f[:, : cols.stop - cols.start],
                        bv[i, r, :, cols].astype(F32),
                    )
        else:
            k = i - matrices
            emb_lion_chunk(pv.at[k], ev.at[k], eu.at[k], en.at[k], factors[0])
        for c in stores[i]:
            c.start()
    for cs in stores:
        for c in cs:
            c.wait()


def last_kernel(which, shares_ref, counts_ref, clip_ref, emb_mom, *rest):
    n = len(which)
    parts, (_, _, emb_up, emb_new, pv, ev, eu, en, isem, osem) = rest[:n], rest[n:]
    source = [emb_peers(-1)[i] for i in which]
    copy = pltpu.make_async_copy
    loads, stores = [], []
    for k in range(n):
        loads += [copy(parts[k], pv.at[k], isem.at[2 * k]), copy(emb_mom.at[source[k]], ev.at[k], isem.at[2 * k + 1])]
        stores += [
            copy(eu.at[k], emb_up.at[source[k]], osem.at[2 * k]),
            copy(en.at[k], emb_new.at[source[k]], osem.at[2 * k + 1]),
        ]
    for c in loads:
        c.start()
    factor = group_factor(0, shares_ref, counts_ref, clip_ref)
    for k in range(n):
        for c in loads[2 * k : 2 * k + 2]:
            c.wait()
        emb_lion_chunk(pv.at[k], ev.at[k], eu.at[k], en.at[k], factor)
        for c in stores[2 * k : 2 * k + 2]:
            c.start()
    for c in stores:
        c.wait()


def emb_send(value, step):
    pairs = [(a * 2 + b, emb_peer(a, b, step, 1)) for a in range(4) for b in range(2)]
    return lax.ppermute(value, DP, pairs)


def on_device(emb_grad, emb_mom, blk_grad, blk_mom, tile_group, clip_rms):
    dp_count = lax.axis_size(DP)
    mp_count = lax.axis_size(MP)
    z, x, c = (lax.axis_index(name) for name in MP)
    groups = clip_rms.shape[0]
    tile_rows, tile_cols = emb_grad.shape
    own_rows = emb_mom.shape[3]
    matrices, block_rows, block_cols = blk_grad.shape
    owner_rows = blk_mom.shape[2]
    row_blocks = tile_group.shape[1] // dp_count
    block_height = block_rows // row_blocks
    emb_t = emb_grad.T
    emb_payload = jax.ShapeDtypeStruct((EMB_ROWS, 128), BF16)
    emb_first = pl.pallas_call(
        functools.partial(emb_first_kernel, own_rows),
        out_shape=(emb_payload,) * len(FIRST),
        in_specs=[ANY],
        out_specs=(ANY,) * len(FIRST),
        scratch_shapes=[
            pltpu.VMEM((len(FIRST), EMB_ROWS, 128), BF16),
            pltpu.VMEM(emb_t.shape, BF16),
            pltpu.SemaphoreType.DMA((7,)),
            pltpu.SemaphoreType.DMA((len(FIRST),)),
        ],
        compiler_params=pltpu.CompilerParams(vmem_limit_bytes=VMEM_BYTES),
        cost_estimate=pl.CostEstimate(flops=2_000_000, bytes_accessed=1_200_000, transcendentals=0),
        name="emb_first",
    )(emb_t)
    packed = pl.pallas_call(
        functools.partial(blk_pack_kernel, groups),
        out_shape=jax.ShapeDtypeStruct((mp_count, BLK_ROWS, 128), BF16),
        in_specs=[SMEM, ANY, ANY],
        out_specs=ANY,
        scratch_shapes=[
            pltpu.VMEM((16, SUM_ROW, 128), BF16),
            pltpu.VMEM((16, BLK_ROWS - SUM_ROW, 128), BF16),
            pltpu.VMEM(blk_grad.shape, BF16),
            pltpu.VMEM(emb_t.shape, BF16),
            pltpu.SemaphoreType.DMA((2,)),
            pltpu.SemaphoreType.DMA((7,)),
            pltpu.SemaphoreType.DMA((2,)),
        ],
        compiler_params=pltpu.CompilerParams(vmem_limit_bytes=VMEM_BYTES),
        cost_estimate=pl.CostEstimate(flops=10_000_000, bytes_accessed=9_000_000, transcendentals=0),
        name="blk_pack",
    )(tile_group, blk_grad, emb_t)
    blk_parts = lax.all_to_all(packed, MP, split_axis=0, concat_axis=0, tiled=True)

    emb_packed = pl.pallas_call(
        emb_pack_kernel,
        out_shape=(emb_payload,) * len(REST),
        in_specs=[ANY],
        out_specs=(ANY,) * len(REST),
        scratch_shapes=[
            pltpu.VMEM((8, EMB_ROWS, 128), BF16),
            pltpu.VMEM(emb_t.shape, BF16),
            pltpu.SemaphoreType.DMA((7,)),
            pltpu.SemaphoreType.DMA((7,)),
        ],
        compiler_params=pltpu.CompilerParams(vmem_limit_bytes=VMEM_BYTES),
        cost_estimate=pl.CostEstimate(flops=10_000_000, bytes_accessed=9_000_000, transcendentals=0),
        name="emb_pack",
    )(emb_t)
    payloads = dict(zip(FIRST + REST, (*emb_first, *emb_packed)))
    emb_parts = [emb_send(payloads[i], EMB_STEPS[i]) for i in range(7)] + [payloads[7]]

    pieces = jnp.sum(blk_parts[:, SUM_ROW, SUM_LANE : SUM_LANE + 3 * groups].astype(F32), axis=0)
    shares = jnp.broadcast_to(pieces, (dp_count, pieces.shape[0]))
    shares = lax.all_to_all(shares, DP, split_axis=0, concat_axis=0, tiled=True)

    labels = jnp.arange(groups, dtype=jnp.int32)
    first = (labels == 0).astype(F32)
    onehot = (tile_group[..., None] == labels).astype(F32)
    counts = jnp.sum(onehot, axis=(0, 1, 2)) * float(block_height * block_cols) + first * float(
        tile_rows * mp_count * tile_cols * dp_count
    )
    blk_mom_t = jnp.transpose(blk_mom, (0, 2, 1, 3))
    emb_mom_t = jnp.transpose(emb_mom.reshape(dp_count, own_rows, tile_cols), (0, 2, 1))
    blk_shape = jax.ShapeDtypeStruct(blk_mom_t.shape, BF16)
    emb_shape = jax.ShapeDtypeStruct(emb_mom_t.shape, BF16)
    mixed = pl.pallas_call(
        mix_kernel,
        out_shape=blk_shape,
        in_specs=[ANY],
        out_specs=ANY,
        scratch_shapes=[
            pltpu.VMEM(packed.shape, BF16),
            pltpu.VMEM((block_cols // 128 + 1, matrices * owner_rows * mp_count, 128), F32),
            pltpu.VMEM(blk_mom_t.shape, BF16),
            pltpu.SemaphoreType.DMA(()),
            pltpu.SemaphoreType.DMA(()),
        ],
        compiler_params=pltpu.CompilerParams(vmem_limit_bytes=VMEM_BYTES),
        cost_estimate=pl.CostEstimate(flops=10_000_000, bytes_accessed=5_000_000, transcendentals=0),
        name="mix",
    )(blk_parts)

    early, late = EARLY, LATE
    n = len(early)
    payload, chunk = (EMB_ROWS, 128), emb_mom_t.shape[1:]
    emb_update, emb_moment, blk_update, blk_moment = pl.pallas_call(
        functools.partial(lion_kernel, early),
        out_shape=(emb_shape, emb_shape, blk_shape, blk_shape),
        in_specs=[SMEM] * 4 + [ANY] * (3 + n),
        out_specs=(ANY,) * 4,
        scratch_shapes=[pltpu.VMEM(blk_mom_t.shape, BF16)] * 2
        + [pltpu.VMEM((n,) + payload, BF16)]
        + [pltpu.VMEM((n,) + chunk, BF16)] * 3
        + [pltpu.VMEM(blk_mom_t.shape, BF16)] * 2
        + [pltpu.SemaphoreType.DMA((2 * (matrices + n),))] * 2,
        compiler_params=pltpu.CompilerParams(vmem_limit_bytes=VMEM_BYTES),
        cost_estimate=pl.CostEstimate(flops=30_000_000, bytes_accessed=25_000_000, transcendentals=0),
        name="lion",
    )(shares, counts, clip_rms, tile_group, mixed, blk_mom_t, emb_mom_t, *[emb_parts[i] for i in early])
    emb_update, emb_moment = pl.pallas_call(
        functools.partial(last_kernel, late),
        out_shape=(emb_shape, emb_shape),
        in_specs=[SMEM] * 3 + [ANY] * (3 + len(late)),
        out_specs=(ANY, ANY),
        scratch_shapes=[pltpu.VMEM((len(late),) + payload, BF16)]
        + [pltpu.VMEM((len(late),) + chunk, BF16)] * 3
        + [pltpu.SemaphoreType.DMA((2 * len(late),))] * 2,
        input_output_aliases={4 + len(late): 0, 5 + len(late): 1},
        compiler_params=pltpu.CompilerParams(vmem_limit_bytes=VMEM_BYTES),
        cost_estimate=pl.CostEstimate(flops=3_000_000, bytes_accessed=2_300_000, transcendentals=0),
        name="last",
    )(shares, counts, clip_rms, emb_mom_t, *[emb_parts[i] for i in late], emb_update, emb_moment)
    emb_update, emb_moment = (
        jnp.transpose(v, (0, 2, 1)).reshape(emb_mom.shape) for v in (emb_update, emb_moment)
    )
    return (
        emb_update,
        emb_moment,
        jnp.transpose(blk_update, (0, 2, 1, 3)),
        jnp.transpose(blk_moment, (0, 2, 1, 3)),
    )


EARLY = (7, 0, 3, 1, 5, 2, 4)
LATE = (6,)
FIRST = (0, 3)
REST = (1, 2, 4, 5, 6, 7)


def solution(mesh):
    torus = Mesh(mesh.devices.reshape(4, 2, 4, 2, 2), DP_MP)
    return jax.shard_map(
        on_device,
        mesh=torus,
        in_specs=(
            P(MP, DP),
            P(MP, None, DP, None, None),
            P(None, DP, MP),
            P(None, None, DP_MP, None),
            P(),
            P(),
        ),
        out_specs=(
            P(MP, None, DP, None, None),
            P(MP, None, DP, None, None),
            P(None, None, DP_MP, None),
            P(None, None, DP_MP, None),
        ),
        check_vma=False,
    )
```

time: 135 us -> 107 us (0.79)
  the two profiles are of different devices: /device:TPU:0 before, /device:TPU:1 now
where the time goes in v2:
time: 107 us; the launch traced here: 106 us
  Pallas kernels  38.3 us (36%)
  waiting for transfers between devices  38 us (36%)
  starting transfers between devices  26 us (24%)
  other arithmetic  2.21 us (2%)
    ppermute x7, waiting for transfers between devices, emb_send(): return lax.ppermute(value, DP, pairs)  26.3 us
    ppermute x7, starting transfers between devices, emb_send(): return lax.ppermute(value, DP, pairs)  14.3 us
    all_to_all x1, waiting for transfers between devices, on_device(): shares = lax.all_to_all(shares, DP, split_axis=0, concat_axis=0, tiled=True)  11.7 us
    pallas_call x1, Pallas kernels, on_device(): pl.pallas_call(functools.partial(lion_kernel, early), out_shape=(emb_shap...  11.5 us
    all_to_all x1, starting transfers between devices, on_device(): lax.all_to_all(packed, MP, split_axis=0, concat_axis=0, tiled=True)  7.76 us
    pallas_call x1, Pallas kernels, on_device(): pl.pallas_call(emb_pack_kernel, out_shape=(emb_payload,) * len(REST), in_...  7.51 us
    pallas_call x1, Pallas kernels, on_device(): pl.pallas_call(functools.partial(blk_pack_kernel, groups), out_shape=jax....  5.71 us
    pallas_call x1, Pallas kernels, on_device(): pl.pallas_call(mix_kernel, out_shape=blk_shape, in_specs=[ANY], out_specs...  5.64 us
  transfers between devices with their start and end apart: 9, of which 3 were waited for; matrix products, arithmetic and copies ran while one was open for 3% of the time, Pallas kernels for 27%

profile of v2, /device:TPU:1, one launch (start us, length us, event | category | flops | bytes accessed | tf_op | source)
XLA Modules:
  0.0 105.9 jit_solution(6959637538972677804)
XLA Ops:
  0.6 5.7 %blk_pack.1 = bf16[16,520,128]{2,1,0:T(8,128)(2,1)} custom-call(s32[2,16,16]{2,1,0:T(8,128)} %label_ref.3, bf16[2,448,1184]{2,1,0:T(8,128)(2,1)} %grad.1, bf16[448,4752]{1,0:T(8,128)(2,1)} %bitcast.18), custom_call_target="tpu_custom_call" | custom-call | flops 10000000 | bytes 9000000 | tf_op jit(solution)/shard_map/blk_pack/pallas_call | solution.py:415
  6.4 7.8 %all-to-all-start = ((bf16[16,520,128]{2,1,0:T(8,128)(2,1)}), bf16[16,520,128]{2,1,0:T(8,128)(2,1)}, u32[]{:S(2)}, u32[]{:S(2)}) async-start(bf16[16,520,128]{2,1,0:T(8,128)(2,1)} %blk_pack.1), calls=%async_computation | async-start | bytes 4259840 | tf_op jit(solution)/shard_map/all_to_all | solution.py:433
  14.1 4.3 %emb_first.1 = (bf16[2080,128]{1,0:T(8,128)(2,1)}, bf16[2080,128]{1,0:T(8,128)(2,1)}) custom-call(bf16[448,4752]{1,0:T(8,128)(2,1)} %bitcast.19), custom_call_target="tpu_custom_call" | custom-call | flops 2000000 | bytes 1200000 | tf_op jit(solution)/shard_map/emb_first/pallas_call | solution.py:400
  18.5 1.9 %collective-permute-start.1 = (bf16[2080,128]{1,0:T(8,128)(2,1)}, bf16[2080,128]{1,0:T(8,128)(2,1)}, u32[]{:S(2)}, u32[]{:S(2)}) collective-permute-start(bf16[2080,128]{1,0:T(8,128)(2,1)} %get-tuple-element.20), channel_id=1, source_target_pairs={{0,16},{16,0},{32,48},{48,32},{64,80},{80,64},{96,112},{112,96},{1... | collective-permute-start | bytes 1597448 | tf_op jit(solution)/shard_map/ppermute | solution.py:384
  20.4 3.5 %collective-permute-start.2 = (bf16[2080,128]{1,0:T(8,128)(2,1)}, bf16[2080,128]{1,0:T(8,128)(2,1)}, u32[]{:S(2)}, u32[]{:S(2)}) collective-permute-start(bf16[2080,128]{1,0:T(8,128)(2,1)} %get-tuple-element.21), channel_id=1, source_target_pairs={{0,64},{16,80},{32,96},{48,112},{64,0},{80,16},{96,32},{112,48},{1... | collective-permute-start | bytes 1597448 | tf_op jit(solution)/shard_map/ppermute | solution.py:384
  23.9 7.5 %emb_pack.1 = (bf16[2080,128]{1,0:T(8,128)(2,1)}, bf16[2080,128]{1,0:T(8,128)(2,1)}, bf16[2080,128]{1,0:T(8,128)(2,1)}, bf16[2080,128]{1,0:T(8,128)(2,1)}, bf16[...) custom-call(bf16[448,4752]{1,0:T(8,128)(2,1)} %bitcast.20), custom_call_target="tpu_custom_call" | custom-call | flops 10000000 | bytes 9000000 | tf_op jit(solution)/shard_map/emb_pack/pallas_call | solution.py:435
  31.4 0.5 collective-permute-start.3
  31.9 2.3 %collective-permute-start.4 = (bf16[2080,128]{1,0:T(8,128)(2,1)}, bf16[2080,128]{1,0:T(8,128)(2,1)}, u32[]{:S(2)}, u32[]{:S(2)}) collective-permute-start(bf16[2080,128]{1,0:T(8,128)(2,1)} %get-tuple-element.23), channel_id=1, source_target_pairs={{0,96},{16,112},{32,0},{48,16},{64,32},{80,48},{96,64},{112,80},{1... | collective-permute-start | bytes 1597448 | tf_op jit(solution)/shard_map/ppermute | solution.py:384
  34.2 0.0 collective-permute-start.5
  34.2 19.4 %collective-permute-done.1.rest_1_ = bf16[2080,128]{1,0:T(8,128)(2,1)} collective-permute-done((bf16[2080,128]{1,0:T(8,128)(2,1)}, bf16[2080,128]{1,0:T(8,128)(2,1)}, u32[]{:S(2)}, u32[]{:S(2)}) %collective-permute-start.1) | collective-permute-done | bytes 532512 | tf_op jit(solution)/shard_map/ppermute | solution.py:384
  53.5 3.2 %collective-permute-start.6 = (bf16[2080,128]{1,0:T(8,128)(2,1)}, bf16[2080,128]{1,0:T(8,128)(2,1)}, u32[]{:S(2)}, u32[]{:S(2)}) collective-permute-start(bf16[2080,128]{1,0:T(8,128)(2,1)} %get-tuple-element.25), channel_id=1, source_target_pairs={{0,80},{16,64},{32,112},{48,96},{64,16},{80,0},{96,48},{112,32},{1... | collective-permute-start | bytes 1597448 | tf_op jit(solution)/shard_map/ppermute | solution.py:384
  56.7 0.0 collective-permute-done.2.rest_2_
  56.7 2.9 %collective-permute-start = (bf16[2080,128]{1,0:T(8,128)(2,1)}, bf16[2080,128]{1,0:T(8,128)(2,1)}, u32[]{:S(2)}, u32[]{:S(2)}) collective-permute-start(bf16[2080,128]{1,0:T(8,128)(2,1)} %get-tuple-element.18), channel_id=1, source_target_pairs={{0,112},{16,96},{32,16},{48,0},{64,48},{80,32},{96,80},{112,64},{1... | collective-permute-start | bytes 1597448 | tf_op jit(solution)/shard_map/ppermute | solution.py:384
  59.6 0.8 convert_reduce_fusion
  60.5 0.5 fusion.1.counts_ref
  61.0 0.0 all-to-all-done.parts
  61.0 0.9 fusion
  61.8 0.6 broadcast_in_dim.2
  62.4 3.9 %all-to-all-start.1 = ((f32[8,1,12]{2,1,0:T(1,128)}), f32[8,1,12]{2,1,0:T(1,128)}, u32[]{:S(2)}, u32[]{:S(2)}) async-start(f32[8,1,12]{2,1,0:T(1,128)} %broadcast_in_dim.2), calls=%async_computation.1 | async-start | bytes 8192 | tf_op jit(solution)/shard_map/all_to_all | solution.py:455
  66.4 5.6 %mix.1.mixed = bf16[2,28,16,1184]{3,2,1,0:T(8,128)(2,1)} custom-call(bf16[16,520,128]{2,1,0:T(8,128)(2,1)} %all-to-all-done.parts), custom_call_target="tpu_custom_call" | custom-call | flops 10000000 | bytes 5000000 | tf_op jit(solution)/shard_map/mix/pallas_call | solution.py:467
  72.0 0.0 collective-permute-done.3.rest_3_
  72.0 0.0 collective-permute-done.4.rest_4_
  72.0 0.0 collective-permute-done.5.rest_5_
  72.1 6.9 %collective-permute-done.6.rest_6_ = bf16[2080,128]{1,0:T(8,128)(2,1)} collective-permute-done((bf16[2080,128]{1,0:T(8,128)(2,1)}, bf16[2080,128]{1,0:T(8,128)(2,1)}, u32[]{:S(2)}, u32[]{:S(2)}) %collective-permute-start.6) | collective-permute-done | bytes 532512 | tf_op jit(solution)/shard_map/ppermute | solution.py:384
  79.0 11.7 %all-to-all-done.1 = f32[8,1,12]{2,1,0:T(1,128)} async-done(((f32[8,1,12]{2,1,0:T(1,128)}), f32[8,1,12]{2,1,0:T(1,128)}, u32[]{:S(2)}, u32[]{:S(2)}) %all-to-all-start.1) | async-done | bytes 416 | tf_op jit(solution)/shard_map/all_to_all | solution.py:455
  90.6 11.5 %lion.1 = (bf16[8,448,594]{2,1,0:T(8,128)(2,1)}, bf16[8,448,594]{2,1,0:T(8,128)(2,1)}, bf16[2,28,16,1184]{3,2,1,0:T(8,128)(2,1)}, bf16[2,28,16,1184]{3,2,1,0:T(8,128)(2,1)}) custom-call(f32[8,12]{1,0:T(8,128)} %bitcast.1.shares_ref, f32[4]{0:T(128)} %fusion.1.counts_ref, f32[4]{0:T(128)} %clip_ref.3, s32[2,16,16]{2,1,0:T(8,128)} %label_ref.3, ...), custom_call_target="tpu_custom_call" | custom-call | flops 30000000 | bytes 25000000 | tf_op jit(solution)/shard_map/lion/pallas_call | solution.py:487
  102.2 0.0 collective-permute-done.rest_0_
  102.2 3.6 %last.1 = (bf16[8,448,594]{2,1,0:T(8,128)(2,1)}, bf16[8,448,594]{2,1,0:T(8,128)(2,1)}) custom-call(f32[8,12]{1,0:T(8,128)} %bitcast.1.shares_ref, f32[4]{0:T(128)} %fusion.1.counts_ref, f32[4]{0:T(128)} %clip_ref.3, bf16[8,448,594]{2,1,0:T(8,128)(2,1)} %bitcast.22, ...), custom_call_target="tpu_custom_call", output_to_operand_aliasing={{0}: (5, {}), {1}: (6, {})} | custom-call | flops 3000000 | bytes 2300000 | tf_op jit(solution)/shard_map/last/pallas_call | solution.py:501
Async XLA Ops:
  6.4 54.6 %all-to-all-start = ((bf16[16,520,128]{2,1,0:T(8,128)(2,1)}), bf16[16,520,128]{2,1,0:T(8,128)(2,1)}, u32[]{:S(2)}, u32[]{:S(2)}) async-start(bf16[16,520,128]{2,1,0:T(8,128)(2,1)} %blk_pack.1), calls=%async_computation | async-start | bytes 4259840 | tf_op jit(solution)/shard_map/all_to_all | solution.py:433
  18.5 35.1 %collective-permute-start.1 = (bf16[2080,128]{1,0:T(8,128)(2,1)}, bf16[2080,128]{1,0:T(8,128)(2,1)}, u32[]{:S(2)}, u32[]{:S(2)}) collective-permute-start(bf16[2080,128]{1,0:T(8,128)(2,1)} %get-tuple-element.20), channel_id=1, source_target_pairs={{0,16},{16,0},{32,48},{48,32},{64,80},{80,64},{96,112},{112,96},{1... | collective-permute-start | bytes 1597448 | tf_op jit(solution)/shard_map/ppermute | solution.py:384
  20.4 36.3 %collective-permute-start.2 = (bf16[2080,128]{1,0:T(8,128)(2,1)}, bf16[2080,128]{1,0:T(8,128)(2,1)}, u32[]{:S(2)}, u32[]{:S(2)}) collective-permute-start(bf16[2080,128]{1,0:T(8,128)(2,1)} %get-tuple-element.21), channel_id=1, source_target_pairs={{0,64},{16,80},{32,96},{48,112},{64,0},{80,16},{96,32},{112,48},{1... | collective-permute-start | bytes 1597448 | tf_op jit(solution)/shard_map/ppermute | solution.py:384
  31.4 40.6 %collective-permute-start.3 = (bf16[2080,128]{1,0:T(8,128)(2,1)}, bf16[2080,128]{1,0:T(8,128)(2,1)}, u32[]{:S(2)}, u32[]{:S(2)}) collective-permute-start(bf16[2080,128]{1,0:T(8,128)(2,1)} %get-tuple-element.22), channel_id=1, source_target_pairs={{0,32},{16,48},{32,64},{48,80},{64,96},{80,112},{96,0},{112,16},{1... | collective-permute-start | bytes 1597448 | tf_op jit(solution)/shard_map/ppermute | solution.py:384
  31.9 40.1 %collective-permute-start.4 = (bf16[2080,128]{1,0:T(8,128)(2,1)}, bf16[2080,128]{1,0:T(8,128)(2,1)}, u32[]{:S(2)}, u32[]{:S(2)}) collective-permute-start(bf16[2080,128]{1,0:T(8,128)(2,1)} %get-tuple-element.23), channel_id=1, source_target_pairs={{0,96},{16,112},{32,0},{48,16},{64,32},{80,48},{96,64},{112,80},{1... | collective-permute-start | bytes 1597448 | tf_op jit(solution)/shard_map/ppermute | solution.py:384
  34.2 37.9 %collective-permute-start.5 = (bf16[2080,128]{1,0:T(8,128)(2,1)}, bf16[2080,128]{1,0:T(8,128)(2,1)}, u32[]{:S(2)}, u32[]{:S(2)}) collective-permute-start(bf16[2080,128]{1,0:T(8,128)(2,1)} %get-tuple-element.24), channel_id=1, source_target_pairs={{0,48},{16,32},{32,80},{48,64},{64,112},{80,96},{96,16},{112,0},{1... | collective-permute-start | bytes 1597448 | tf_op jit(solution)/shard_map/ppermute | solution.py:384
  53.5 25.5 %collective-permute-start.6 = (bf16[2080,128]{1,0:T(8,128)(2,1)}, bf16[2080,128]{1,0:T(8,128)(2,1)}, u32[]{:S(2)}, u32[]{:S(2)}) collective-permute-start(bf16[2080,128]{1,0:T(8,128)(2,1)} %get-tuple-element.25), channel_id=1, source_target_pairs={{0,80},{16,64},{32,112},{48,96},{64,16},{80,0},{96,48},{112,32},{1... | collective-permute-start | bytes 1597448 | tf_op jit(solution)/shard_map/ppermute | solution.py:384
  56.7 45.5 %collective-permute-start = (bf16[2080,128]{1,0:T(8,128)(2,1)}, bf16[2080,128]{1,0:T(8,128)(2,1)}, u32[]{:S(2)}, u32[]{:S(2)}) collective-permute-start(bf16[2080,128]{1,0:T(8,128)(2,1)} %get-tuple-element.18), channel_id=1, source_target_pairs={{0,112},{16,96},{32,16},{48,0},{64,48},{80,32},{96,80},{112,64},{1... | collective-permute-start | bytes 1597448 | tf_op jit(solution)/shard_map/ppermute | solution.py:384
  62.4 28.2 %all-to-all-start.1 = ((f32[8,1,12]{2,1,0:T(1,128)}), f32[8,1,12]{2,1,0:T(1,128)}, u32[]{:S(2)}, u32[]{:S(2)}) async-start(f32[8,1,12]{2,1,0:T(1,128)} %broadcast_in_dim.2), calls=%async_computation.1 | async-start | bytes 8192 | tf_op jit(solution)/shard_map/all_to_all | solution.py:455
